TPU v7x, 32 devices: a whole 2x2x4 slice. The times are simulated.
32 devices in a mesh: rep: 4 (over x, y), dp: 8 (over z, core).
Axes of the slice: x: 2, y: 2, z: 4, core: 2. Of those that a mesh axis runs over, the one named last changes fastest.
Arguments:
- x: bfloat16 [32, 2048, 896], P(('rep', 'dp')), parts along dimension 0
- dy: bfloat16 [32, 2048, 896], P(('rep', 'dp')), parts along dimension 0
- w_gate: bfloat16 [2, 896, 2304], replicated
- w_up: bfloat16 [2, 896, 2304], replicated
- w_down: bfloat16 [2, 2304, 896], replicated
- m_w_gate: float32 [2, 896, 2304], P(None, 'dp')
- m_w_up: float32 [2, 896, 2304], P(None, 'dp')
- m_w_down: float32 [2, 2304, 896], P(None, 'dp')
- v_w_gate: float32 [2, 896, 2304], P(None, 'dp')
- v_w_up: float32 [2, 896, 2304], P(None, 'dp')
- v_w_down: float32 [2, 2304, 896], P(None, 'dp')
Outputs:
- output 1: bfloat16 [8, 896, 2304], P('rep'), parts along dimension 0
- output 2: bfloat16 [8, 896, 2304], P('rep'), parts along dimension 0
- output 3: bfloat16 [8, 2304, 896], P('rep'), parts along dimension 0
- output 4: float32 [8, 896, 2304], P('rep', 'dp'), parts along dimension 0
- output 5: float32 [8, 896, 2304], P('rep', 'dp'), parts along dimension 0
- output 6: float32 [8, 2304, 896], P('rep', 'dp'), parts along dimension 0
- output 7: float32 [8, 896, 2304], P('rep', 'dp'), parts along dimension 0
- output 8: float32 [8, 896, 2304], P('rep', 'dp'), parts along dimension 0
- output 9: float32 [8, 2304, 896], P('rep', 'dp'), parts along dimension 0
There are 4 independent parts. A program takes and returns all parts, laid end to end along the dimension named above; an argument that names none is the same for every part.
All inputs are finite; a program needn't handle non-finite values.
Results may differ from a plain program's by a relative error of at most 0.02.
Values are sent between devices in bfloat16 or wider.
A program may use at most 2 GiB of HBM per device.

v0:
```python
import jax
import jax.numpy as jnp
from jax import lax

NAMES = ("w_gate", "w_up", "w_down")


def matmul(a, w):
    return jnp.dot(a, w, preferred_element_type=jnp.float32).astype(jnp.bfloat16)


def normed(h):
    wide = h.astype(jnp.float32)
    scale = lax.rsqrt(jnp.mean(wide**2, -1, keepdims=True) + 1e-6)
    return (wide * scale).astype(jnp.bfloat16)


def layer(h, w):
    a = normed(h)
    gate = jnp.dot(a, w["w_gate"], preferred_element_type=jnp.float32)
    up = jnp.dot(a, w["w_up"], preferred_element_type=jnp.float32)
    return h + matmul((jax.nn.silu(gate) * up).astype(jnp.bfloat16), w["w_down"])


def adamw(w, m, v, g):
    m = 0.9 * m + 0.1 * g
    v = 0.95 * v + 0.05 * g * g
    step = m * lax.rsqrt(v + 1e-8) + 0.1 * w
    return (w - 0.02 * step).astype(jnp.bfloat16), m, v


def stack(weights, h):
    for number in range(weights["w_gate"].shape[0]):
        h = layer(h, {name: w[number] for name, w in weights.items()})
    return h


def solution(mesh):
    groups = mesh.shape["rep"]

    def step(x, dy, *arrays):
        weights, m, v = (arrays[i : i + 3] for i in (0, 3, 6))
        x, dy = (t.reshape(groups, -1, *t.shape[1:]) for t in (x, dy))

        def of_a_group(x, dy):
            _, back = jax.vjp(lambda w: stack(w, x), dict(zip(NAMES, weights, strict=True)))
            by_weights = back(dy)[0]
            gradients = [by_weights[name].astype(jnp.float32) for name in NAMES]
            new = [adamw(w.astype(jnp.float32), m, v, g) for w, m, v, g in zip(weights, m, v, gradients, strict=True)]
            return tuple(one[which] for which in range(3) for one in new)

        return tuple(t.reshape(-1, *t.shape[2:]) for t in jax.vmap(of_a_group)(x, dy))

    return step
```

profile of v0, /device:TPU:0, one launch (start us, length us, event | category | flops | bytes accessed | tf_op | source)
XLA Modules:
  0.0 1013.9 jit_solution(14469566388434276220)
XLA Ops:
  10.0 6.2 copy
  16.2 13.7 %fusion.65 = f32[2048,2304]{1,0:T(8,128)S(1)} fusion(bf16[2,896,2304]{2,1,0:T(8,128)(2,1)} %param, bf16[1,2048,896]{2,1,0:T(8,128)(2,1)} %param.2, f32[2048]{0:T(1024)S(1)} %add_rsqrt_fusion), kind=kOutput, calls=%fused_computation.77 | convolution fusion | flops 8461221888 | bytes 26681344 | tf_op jit(solution)/vmap(jvp())/dot_general | solution.py:20
  29.9 18.8 %fusion.63 = f32[2048,2304]{1,0:T(8,128)} fusion(bf16[2,896,2304]{2,1,0:T(8,128)(2,1)} %param.3, bf16[1,2048,896]{2,1,0:T(8,128)(2,1)S(1)} %copy-done.1, f32[2048]{0:T(1024)S(1)} %add_rsqrt_fusion), kind=kOutput, calls=%fused_computation.75 | convolution fusion | flops 8461221888 | bytes 26681344 | tf_op jit(solution)/vmap(jvp())/dot_general | solution.py:21
  48.8 14.0 %fusion.28 = bf16[2048,2304]{1,0:T(8,128)(2,1)} fusion(f32[2048,2304]{1,0:T(8,128)} %fusion.63, f32[2048,2304]{1,0:T(8,128)S(1)} %fusion.65), kind=kLoop, calls=%fused_computation.43 | loop fusion | flops 28311552 | bytes 47185920
  62.8 13.2 %fusion.37 = (f32[2048]{0:T(1024)S(1)}, bf16[1,1,2048,896]{2,3,1,0:T(8,128)(2,1)S(1)}) fusion(bf16[2048,2304]{1,0:T(8,128)(2,1)} %fusion.28, bf16[2,2304,896]{2,1,0:T(8,128)(2,1)} %param.4, bf16[1,2048,896]{1,2,0:T(8,128)(2,1)S(1)} %copy-done.4), kind=kOutput, calls=%fused_computation.54 | convolution fusion | flops 8464889856 | bytes 20914176 | tf_op jit(solution)/vmap(jvp())/dot_general | solution.py:9
  76.1 16.4 %fusion.52 = f32[2048,2304]{1,0:T(8,128)} fusion(bf16[2,896,2304]{2,1,0:T(8,128)(2,1)} %param, bf16[1,1,2048,896]{2,3,1,0:T(8,128)(2,1)S(1)} %get-tuple-element.10, f32[2048]{0:T(1024)S(1)} %bitcast.324), kind=kOutput, calls=%fused_computation.64 | convolution fusion | flops 8461221888 | bytes 26681344 | tf_op jit(solution)/vmap(jvp())/dot_general | solution.py:20
  92.5 15.2 %fusion.56 = f32[2048,2304]{1,0:T(8,128)} fusion(bf16[2,896,2304]{2,1,0:T(8,128)(2,1)} %param.3, bf16[1,1,2048,896]{2,3,1,0:T(8,128)(2,1)S(1)} %get-tuple-element.10, f32[2048]{0:T(1024)S(1)} %bitcast.325), kind=kOutput, calls=%fused_computation.68 | convolution fusion | flops 8461221888 | bytes 26681344 | tf_op jit(solution)/vmap(jvp())/dot_general | solution.py:21
  107.7 12.6 %fusion.26 = bf16[1,1,2048,2304]{3,2,1,0:T(8,128)(2,1)} fusion(bf16[2,2304,896]{2,1,0:T(8,128)(2,1)S(1)} %bitcast.320, bf16[1,2048,896]{2,1,0:T(8,128)(2,1)S(1)} %copy-done.3), kind=kOutput, calls=%fused_computation.41 | convolution fusion | flops 8460435456 | bytes 17235968 | tf_op jit(solution)/vmap(transpose(jvp()))/dot_general | solution.py:9
  120.3 6.0 copy.1
  126.3 16.4 %fusion.6 = bf16[2048,2304]{1,0:T(8,128)(2,1)S(1)} fusion(f32[2048,2304]{1,0:T(8,128)} %fusion.52, f32[2048,2304]{1,0:T(8,128)} %fusion.56, bf16[1,1,2048,2304]{3,2,1,0:T(8,128)(2,1)} %fusion.26), kind=kLoop, calls=%fused_computation.11 | loop fusion | flops 56623104 | bytes 56623104
  146.4 11.7 %fusion.54 = bf16[2048,896]{0,1:T(8,128)(2,1)} fusion(bf16[2048,2304]{1,0:T(8,128)(2,1)S(1)} %fusion.6, bf16[2,896,2304]{2,1,0:T(8,128)(2,1)} %param), kind=kOutput, calls=%fused_computation.66 | convolution fusion | flops 8455716864 | bytes 17235968 | tf_op jit(solution)/vmap(transpose(jvp()))/dot_general | solution.py:20
  158.1 21.1 %fusion.39 = (f32[2048]{0:T(1024)S(1)}, bf16[2048,896]{0,1:T(8,128)(2,1)}) fusion(bf16[1,1,2048,896]{2,3,1,0:T(8,128)(2,1)} %copy-done.6, bf16[2048,896]{0,1:T(8,128)(2,1)} %fusion.54, bf16[2,896,2304]{2,1,0:T(8,128)(2,1)} %param.3, bf16[1,1,2048,2304]{3,2,1,0:T(8,128)(2,1)} %fusion.26, f32[2048,2304]{1,0:T(8,128)} %fusion.52), kind=kOutput, calls=%fused_computation.56 | convolution fusion | flops 8495036416 | bytes 43458560 | tf_op jit(solution)/vmap(transpose(jvp()))/dot_general | solution.py:21
  179.3 6.9 fusion.73
  188.0 15.0 %convolution_bitcast_fusion = f32[1,2304,896]{2,1,0:T(8,128)} fusion(bf16[2048,2304]{1,0:T(8,128)(2,1)} %fusion.28, bf16[2048,896]{0,1:T(8,128)(2,1)S(1)} %fusion.73), kind=kOutput, calls=%fused_computation.62 | convolution fusion | flops 8455716864 | bytes 21364736 | tf_op jit(solution)/vmap(transpose(jvp()))/dot_general | solution.py:9
  203.1 20.0 %fusion.40 = f32[1,2304,896]{2,1,0:T(8,128)} fusion(f32[2048,2304]{1,0:T(8,128)} %fusion.56, f32[2048,2304]{1,0:T(8,128)} %fusion.52, bf16[1,2048,896]{2,1,0:T(8,128)(2,1)} %param.5), kind=kOutput, calls=%fused_computation.58 | convolution fusion | flops 8484028416 | bytes 49676288 | tf_op jit(solution)/vmap(transpose(jvp()))/dot_general | solution.py:9
  223.2 15.4 %fusion.27 = bf16[1,1,2048,2304]{3,2,1,0:T(8,128)(2,1)} fusion(bf16[2048,896]{0,1:T(8,128)(2,1)} %copy-done.7, bf16[2,2304,896]{2,1,0:T(8,128)(2,1)} %param.4), kind=kOutput, calls=%fused_computation.42 | convolution fusion | flops 8460435456 | bytes 17235968 | tf_op jit(solution)/vmap(transpose(jvp()))/dot_general | solution.py:9
  238.6 17.6 %fusion.49 = f32[1,896,2304]{2,1,0:T(8,128)} fusion(bf16[1,1,2048,2304]{3,2,1,0:T(8,128)(2,1)} %fusion.27, f32[2048,2304]{1,0:T(8,128)} %copy-done, bf16[1,2048,896]{1,2,0:T(8,128)(2,1)S(1)} %copy-done.5, f32[2048]{0:T(1024)S(1)} %copy-done.11), kind=kOutput, calls=%fused_computation.61 | convolution fusion | flops 8489533440 | bytes 40247296 | tf_op jit(solution)/vmap(transpose(jvp()))/dot_general | solution.py:21
  256.3 18.8 %fusion.43 = f32[1,896,2304]{2,1,0:T(8,128)} fusion(bf16[1,1,2048,2304]{3,2,1,0:T(8,128)(2,1)} %fusion.26, f32[2048,2304]{1,0:T(8,128)} %fusion.52, bf16[1,1,2048,896]{2,3,1,0:T(8,128)(2,1)} %copy-done.6, f32[2048]{0:T(1024)S(1)} %bitcast.327), kind=kOutput, calls=%fused_computation.59 | convolution fusion | flops 8489533440 | bytes 40247296 | tf_op jit(solution)/vmap(transpose(jvp()))/dot_general | solution.py:21
  275.2 15.1 %convolution_bitcast_fusion.1 = f32[1,896,2304]{2,1,0:T(8,128)} fusion(bf16[2048,2304]{1,0:T(8,128)(2,1)} %copy-done.2, bf16[1,1,2048,896]{2,3,1,0:T(8,128)(2,1)} %copy-done.6, f32[2048]{0:T(1024)S(1)} %bitcast.328), kind=kOutput, calls=%fused_computation.63 | convolution fusion | flops 8461221888 | bytes 21372928 | tf_op jit(solution)/vmap(transpose(jvp()))/dot_general | solution.py:20
  290.4 25.2 %fusion.46 = f32[1,896,2304]{2,1,0:T(8,128)} fusion(f32[2048,2304]{1,0:T(8,128)} %copy-done, f32[2048,2304]{1,0:T(8,128)} %fusion.63, bf16[1,1,2048,2304]{3,2,1,0:T(8,128)(2,1)} %fusion.27, bf16[1,2048,896]{1,2,0:T(8,128)(2,1)} %copy, f32[2048]{0:T(1024)S(1)} %copy-done.11), kind=kOutput, calls=%fused_computation.60 | convolution fusion | flops 8513126400 | bytes 59121664 | tf_op jit(solution)/vmap(transpose(jvp()))/dot_general | solution.py:20
  318.8 64.4 %reduce-scatter.27.cloned.1.call-done = f32[1,288,896]{2,1,0:T(8,128)} async-done(((f32[1,2304,896]{2,1,0:T(8,128)}), f32[1,288,896]{2,1,0:T(8,128)}) %reduce-scatter.27.cloned.1.call-update) | async-done | bytes 1032208
  389.9 83.1 %reduce-scatter.25.cloned.1.call-done = f32[1,112,2304]{2,1,0:T(8,128)} async-done(((f32[1,896,2304]{2,1,0:T(8,128)}), f32[1,112,2304]{2,1,0:T(8,128)}) %reduce-scatter.25.cloned.1.call-update) | async-done | bytes 1032208
  474.3 87.8 %reduce-scatter.23.cloned.1.call-done = f32[1,112,2304]{2,1,0:T(8,128)} async-done(((f32[1,896,2304]{2,1,0:T(8,128)}), f32[1,112,2304]{2,1,0:T(8,128)}) %reduce-scatter.23.cloned.1.call-update) | async-done | bytes 1032208
  563.4 6.0 fusion.122
  569.5 82.2 %reduce-scatter.19.cloned.1.call-done = f32[1,112,2304]{2,1,0:T(8,128)} async-done(((f32[1,896,2304]{2,1,0:T(8,128)}), f32[1,112,2304]{2,1,0:T(8,128)}) %reduce-scatter.19.cloned.1.call-update) | async-done | bytes 1032208
  653.0 88.4 %reduce-scatter.21.cloned.1.call-done = f32[1,112,2304]{2,1,0:T(8,128)} async-done(((f32[1,896,2304]{2,1,0:T(8,128)}), f32[1,112,2304]{2,1,0:T(8,128)}) %reduce-scatter.21.cloned.1.call-update) | async-done | bytes 1032208
  748.0 74.2 %all-gather.14.cloned.1.call-done = bf16[1,2,2304,896]{3,2,1,0:T(8,128)(2,1)} async-done(((bf16[1,2,288,896]{3,2,1,0:T(8,128)(2,1)}), bf16[1,2,2304,896]{3,2,1,0:T(8,128)(2,1)}) %all-gather.14.cloned.1.call-update) | async-done | bytes 8257552 | tf_op jit(solution)/reshape | solution.py:52
  822.1 81.5 %all-gather.12.cloned.1.call-done = bf16[1,2,896,2304]{3,2,1,0:T(8,128)(2,1)} async-done(((bf16[1,2,112,2304]{3,2,1,0:T(8,128)(2,1)}), bf16[1,2,896,2304]{3,2,1,0:T(8,128)(2,1)}) %all-gather.12.cloned.1.call-update) | async-done | bytes 8257552 | tf_op jit(solution)/reshape | solution.py:52
  903.6 81.5 %all-gather.10.cloned.1.call-done = bf16[1,2,896,2304]{3,2,1,0:T(8,128)(2,1)} async-done(((bf16[1,2,112,2304]{3,2,1,0:T(8,128)(2,1)}), bf16[1,2,896,2304]{3,2,1,0:T(8,128)(2,1)}) %all-gather.10.cloned.1.call-update) | async-done | bytes 8257552 | tf_op jit(solution)/reshape | solution.py:52
  985.1 7.2 copy.5
  992.3 7.2 copy.6
  999.5 7.3 copy.7
  (64 shorter events, 28.4 us)
Async XLA Ops:
  7.2 310.4 %reduce-scatter.29.cloned.1.call-start = ((), (), s32[]{:S(2)}) async-start(), calls=%async_computation.14 | async-start | bytes 9289728
  16.2 13.7 %copy-start.10 = (f32[2048]{0:T(1024)}, f32[2048]{0:T(1024)S(1)}, u32[]{:S(2)}) copy-start(f32[2048]{0:T(1024)S(1)} %add_rsqrt_fusion) | copy-start | bytes 24580
  16.2 13.7 %copy-start.1 = (bf16[1,2048,896]{2,1,0:T(8,128)(2,1)S(1)}, bf16[1,2048,896]{2,1,0:T(8,128)(2,1)}, u32[]{:S(2)}) copy-start(bf16[1,2048,896]{2,1,0:T(8,128)(2,1)} %param.2) | copy-start | bytes 11010052
  29.9 18.8 %copy-start = (f32[2048,2304]{1,0:T(8,128)}, f32[2048,2304]{1,0:T(8,128)S(1)}, u32[]{:S(2)}) copy-start(f32[2048,2304]{1,0:T(8,128)S(1)} %fusion.65) | copy-start | bytes 56623108
  48.8 14.0 %copy-start.4 = (bf16[1,2048,896]{1,2,0:T(8,128)(2,1)S(1)}, bf16[1,2048,896]{1,2,0:T(8,128)(2,1)}, u32[]{:S(2)}) copy-start(bf16[1,2048,896]{1,2,0:T(8,128)(2,1)} %copy) | copy-start | bytes 11010052
  76.0 16.5 %copy-start.6 = (bf16[1,1,2048,896]{2,3,1,0:T(8,128)(2,1)}, bf16[1,1,2048,896]{2,3,1,0:T(8,128)(2,1)S(1)}, u32[]{:S(2)}) copy-start(bf16[1,1,2048,896]{2,3,1,0:T(8,128)(2,1)S(1)} %get-tuple-element.10) | copy-start | bytes 11010052
  76.1 31.6 %slice-start = ((s8[8257536]{0:T(1024)(128)(4,1)}), s8[4194304]{0:T(1024)(128)(4,1)S(1)}, s32[]{:S(2)}) async-start(s8[8257536]{0:T(1024)(128)(4,1)} %bitcast.319), calls=%async_computation.15 | async-start | bytes 8388608
  92.5 15.2 %copy-start.3 = (bf16[1,2048,896]{2,1,0:T(8,128)(2,1)S(1)}, bf16[1,2048,896]{2,1,0:T(8,128)(2,1)}, u32[]{:S(2)}) copy-start(bf16[1,2048,896]{2,1,0:T(8,128)(2,1)} %param.5) | copy-start | bytes 11010052
  92.5 15.2 %slice-start.1 = ((s8[8257536]{0:T(1024)(128)(4,1)}), s8[4063232]{0:T(1024)(128)(4,1)S(1)}, s32[]{:S(2)}) async-start(s8[8257536]{0:T(1024)(128)(4,1)} %bitcast.319), calls=%async_computation.16 | async-start | bytes 8126464
  142.7 3.7 copy-start.2
  186.1 1.8 copy-start.7
  203.0 180.2 %reduce-scatter.27.cloned.1.call-start = ((), (), s32[]{:S(2)}) async-start(), calls=%async_computation.13 | async-start | bytes 9289728
  223.1 15.5 %copy-start.11 = (f32[2048]{0:T(1024)S(1)}, f32[2048]{0:T(1024)}, u32[]{:S(2)}) copy-start(f32[2048]{0:T(1024)} %copy-done.10) | copy-start | bytes 24580
  223.1 249.9 %reduce-scatter.25.cloned.1.call-start = ((), (), s32[]{:S(2)}) async-start(), calls=%async_computation.12 | async-start | bytes 9289728
  223.2 15.4 %copy-start.5 = (bf16[1,2048,896]{1,2,0:T(8,128)(2,1)S(1)}, bf16[1,2048,896]{1,2,0:T(8,128)(2,1)}, u32[]{:S(2)}) copy-start(bf16[1,2048,896]{1,2,0:T(8,128)(2,1)} %copy) | copy-start | bytes 11010052
  256.2 305.9 %reduce-scatter.23.cloned.1.call-start = ((), (), s32[]{:S(2)}) async-start(), calls=%async_computation.11 | async-start | bytes 9289728
  275.1 376.6 %reduce-scatter.19.cloned.1.call-start = ((), (), s32[]{:S(2)}) async-start(), calls=%async_computation.9 | async-start | bytes 9289728
  290.3 451.0 %reduce-scatter.21.cloned.1.call-start = ((), (), s32[]{:S(2)}) async-start(), calls=%async_computation.10 | async-start | bytes 9289728
  315.6 0.7 copy-start.12
  315.6 68.9 %copy-start.8 = (f32[2,288,896]{2,1,0:T(8,128)S(1)}, f32[2,288,896]{2,1,0:T(8,128)}, u32[]{:S(2)}) copy-start(f32[2,288,896]{2,1,0:T(8,128)} %param.10) | copy-start | bytes 6193156
  315.6 506.5 %all-gather.14.cloned.1.call-start = ((), (), s32[]{:S(2)}) async-start(), calls=%async_computation.8 | async-start | bytes 9289728 | tf_op jit(solution)/reshape | solution.py:52
  389.8 513.8 %all-gather.12.cloned.1.call-start = ((), (), s32[]{:S(2)}) async-start(), calls=%async_computation.7 | async-start | bytes 9289728 | tf_op jit(solution)/reshape | solution.py:52
  563.4 179.3 %copy-start.9 = (f32[2,112,2304]{2,1,0:T(8,128)S(1)}, f32[2,112,2304]{2,1,0:T(8,128)}, u32[]{:S(2)}) copy-start(f32[2,112,2304]{2,1,0:T(8,128)} %param.6) | copy-start | bytes 6193156
  569.4 415.6 %all-gather.10.cloned.1.call-start = ((), (), s32[]{:S(2)}) async-start(), calls=%async_computation.6 | async-start | bytes 9289728 | tf_op jit(solution)/reshape | solution.py:52
Sparse Core Ops, SparseCore 0:
  203.1 90.8 reduce-scatter.28
  296.3 86.8 reduce-scatter.26
  386.1 86.8 reduce-scatter.24
  475.2 86.8 reduce-scatter.22
  564.8 86.8 reduce-scatter.18
  654.5 86.8 reduce-scatter.20
  743.0 79.1 all-gather.13
  824.3 79.2 all-gather.11
  905.8 79.2 all-gather.9
where the time goes:
time: 1020 us; the launch traced here: 1010 us
  waiting for transfers between devices  643 us (63%)
  matrix products  250 us (25%)
  other arithmetic  64.5 us (6%)
  local copies, waits for them, and re-layouts  40.7 us (4%)
  between operations  15.2 us (1%)
    unnamed x15, waiting for transfers between devices  406 us
    reshape x3, waiting for transfers between devices, step(): t.reshape(-1, *t.shape[2:])  237 us
    dot_general x5, matrix products, layer(): up = jnp.dot(a, w['w_up'], preferred_element_type=jnp.float32)  91.6 us
    dot_general x5, matrix products, layer(): gate = jnp.dot(a, w['w_gate'], preferred_element_type=jnp.float32)  82.1 us
    dot_general x5, matrix products, matmul(): jnp.dot(a, w, preferred_element_type=jnp.float32).astype(jnp.bfloat16)  76.2 us
    unnamed x35, local copies, waits for them, and re-layouts  40.1 us
    unnamed x4, other arithmetic  37.3 us
  transfers between devices with their start and end apart: 9, of which 8 were waited for; matrix products, arithmetic and copies ran while one was open for 14% of the time, Pallas kernels for 0%

commit v1 on v0

v1 whole, which is shorter than its diff:
```python
import functools

import jax
import jax.numpy as jnp
from jax import lax
from jax.experimental import pallas as pl
from jax.experimental.pallas import tpu as pltpu
from jax.sharding import PartitionSpec as P

MESH = pl.DeviceIdType.MESH
F32, BF16 = jnp.float32, jnp.bfloat16
T, D, FF = 2048, 896, 2304
CF = 256
STEPS = FF // CF
RB = 512
NRB = T // RB
ROWS = 224
PER_LAYER = 27
Q = 2 * PER_LAYER
RING = 12
SENDS = 4
LAST = Q + 18
VMEM_LIMIT = 67043328


def nt(a, b):
    return lax.dot_general(a, b, (((1,), (1,)), ((), ())), preferred_element_type=F32)


def nn(a, b):
    return jnp.dot(a, b, preferred_element_type=F32)


def norm_scale(wide):
    return lax.rsqrt(jnp.mean(wide * wide, -1, keepdims=True) + 1e-6)


def sigmoid(g):
    return 1.0 / (1.0 + jnp.exp(-g))


def forward_kernel(x, wg, wu, wd, g_out, u_out, hid_t, a0_t, h1, a1, a1_t, acc, a0):
    j = pl.program_id(0)

    @pl.when(j == 0)
    def _():
        @pl.loop(0, NRB)
        def _(r):
            rows = pl.ds(pl.multiple_of(r * RB, RB), RB)
            wide = x[rows, :].astype(F32)
            a = (wide * norm_scale(wide)).astype(BF16)
            a0[rows, :] = a
            a0_t[:, rows] = a.T

    @pl.loop(0, NRB)
    def _(r):
        rows = pl.ds(pl.multiple_of(r * RB, RB), RB)
        a = a0[rows, :]
        g = nn(a, wg[0])
        u = nn(a, wu[0])
        g_out[0, rows, :] = g
        u_out[0, rows, :] = u
        hid = (g * sigmoid(g) * u).astype(BF16)
        hid_t[:, :, rows] = hid.T.reshape(8, 32, RB)
        y = nn(hid, wd[0])

        @pl.when(j == 0)
        def _():
            acc[rows, :] = y

        @pl.when(j > 0)
        def _():
            acc[rows, :] += y

    @pl.when(j == STEPS - 1)
    def _():
        @pl.loop(0, NRB)
        def _(r):
            rows = pl.ds(pl.multiple_of(r * RB, RB), RB)
            y = acc[rows, :].astype(BF16).astype(F32)
            h = (x[rows, :].astype(F32) + y).astype(BF16)
            h1[rows, :] = h
            wide = h.astype(F32)
            a = (wide * norm_scale(wide)).astype(BF16)
            a1[rows, :] = a
            a1_t[:, rows] = a.T


def forward(x, wg, wu, wd):
    whole = lambda *shape: pl.BlockSpec(shape, lambda j: (0,) * len(shape), pipeline_mode=pl.Buffered(1))
    step = lambda *shape: pl.BlockSpec(shape, lambda j: (j,) + (0,) * (len(shape) - 1))
    return pl.pallas_call(
        forward_kernel,
        grid=(STEPS,),
        in_specs=[
            whole(T, D),
            pl.BlockSpec((1, D, CF), lambda j: (0, 0, j)),
            pl.BlockSpec((1, D, CF), lambda j: (0, 0, j)),
            pl.BlockSpec((1, CF, D), lambda j: (0, j, 0)),
        ],
        out_specs=[step(1, T, CF), step(1, T, CF), step(8, 32, T), whole(D, T), whole(T, D), whole(T, D), whole(D, T)],
        out_shape=[
            jax.ShapeDtypeStruct((STEPS, T, CF), F32),
            jax.ShapeDtypeStruct((STEPS, T, CF), F32),
            jax.ShapeDtypeStruct((72, 32, T), BF16),
            jax.ShapeDtypeStruct((D, T), BF16),
            jax.ShapeDtypeStruct((T, D), BF16),
            jax.ShapeDtypeStruct((T, D), BF16),
            jax.ShapeDtypeStruct((D, T), BF16),
        ],
        scratch_shapes=[pltpu.VMEM((T, D), F32), pltpu.VMEM((T, D), BF16)],
        compiler_params=pltpu.CompilerParams(vmem_limit_bytes=VMEM_LIMIT, dimension_semantics=("arbitrary",)),
        name="forward0",
    )(x, wg, wu, wd)


def train_kernel(
    wg, wu, wd, mg, mu, md, vg, vu, vd, dy, h1, a1, a1_t, a0_t, hid0_t, g0, u0,
    wtmp, gown, hid1_t,
    dyv, av, at, gbuf, ubuf, dg, du, wgj, wuj, wdj, hid_b, hid_c, dag, dau,
    grad, pin, rin, lin, rout, lout, wown, gownb, gfin, mb, vb, wb, mbd, vbd, wbd,
    load_sem, w_sem, gu_sem, hw_sem, hc_sem,
    p_send, p_recv, r_send, r_recv, l_send, l_recv,
    ar_send, ar_recv, al_send, al_recv, ap_send, ap_recv, wo_sem, go_sem, ad_sem,
):
    rep, me = lax.axis_index("rep"), lax.axis_index("dp")
    z, c = me // 2, me % 2
    partner = (rep, z * 2 + (1 - c))
    right = (rep, jnp.minimum(z + 1, 3) * 2 + c)
    left = (rep, jnp.maximum(z - 1, 0) * 2 + c)

    bar = pltpu.get_barrier_semaphore()
    pl.semaphore_signal(bar, inc=1, device_id=partner, device_id_type=MESH)

    @pl.when(z < 3)
    def _():
        pl.semaphore_signal(bar, inc=1, device_id=right, device_id_type=MESH)

    @pl.when(z > 0)
    def _():
        pl.semaphore_signal(bar, inc=1, device_id=left, device_id_type=MESH)

    @pl.when((z == 0) | (z == 3))
    def _():
        pl.semaphore_wait(bar, 2)

    @pl.when((z > 0) & (z < 3))
    def _():
        pl.semaphore_wait(bar, 3)

    valid = lambda q: (q >= 0) & (q < Q)

    def remote(src, dst, send, recv, to):
        return pltpu.make_async_remote_copy(
            src_ref=src, dst_ref=dst, send_sem=send, recv_sem=recv, device_id=to, device_id_type=MESH
        )

    def to_partner(q):
        return remote(grad.at[q % RING, 1 - c], pin.at[q % RING], p_send.at[q % SENDS], p_recv.at[q % RING], partner)

    def sum_right(q, frm):
        part = pl.ds(frm + 1, 3 - frm)
        return remote(rout.at[q % SENDS, part], rin.at[q % RING, part], r_send.at[q % SENDS], r_recv.at[q % RING], right)

    def sum_left(q, frm):
        part = pl.ds(0, frm)
        return remote(lout.at[q % SENDS, part], lin.at[q % RING, part], l_send.at[q % SENDS], l_recv.at[q % RING], left)

    def new_right(q, frm):
        part = pl.ds(0, frm + 1)
        here = wtmp.at[q, c, part]
        return remote(here, here, ar_send.at[q % SENDS], ar_recv.at[q % RING], right)

    def new_left(q, frm):
        part = pl.ds(frm, 4 - frm)
        here = wtmp.at[q, c, part]
        return remote(here, here, al_send.at[q % SENDS], al_recv.at[q % RING], left)

    def new_partner(q, core):
        here = wtmp.at[q, core]
        return remote(here, here, ap_send.at[q % SENDS], ap_recv.at[q % RING], partner)

    def keep_new(q):
        return pltpu.make_async_copy(wown.at[q % SENDS], wtmp.at[q, c, z], wo_sem.at[q % SENDS])

    def keep_grad(q):
        return pltpu.make_async_copy(gownb.at[q % SENDS], gown.at[q], go_sem.at[q % SENDS])

    def moments(q, act):
        layer = jnp.where(q < PER_LAYER, 1, 0)
        n = q % PER_LAYER
        s = q % 2
        cols = pl.ds(pl.multiple_of((n // 2) * CF, CF), CF)
        for which, (m, v, w) in enumerate(((mg, vg, wg), (mu, vu, wu))):

            @pl.when((n < 18) & (n % 2 == which))
            def _():
                own = pl.ds(pl.multiple_of(me * 112, 16), 112)
                act(pltpu.make_async_copy(m.at[layer, :, cols], mb.at[s], ad_sem.at[s, 0]))
                act(pltpu.make_async_copy(v.at[layer, :, cols], vb.at[s], ad_sem.at[s, 1]))
                act(pltpu.make_async_copy(w.at[layer, own, cols], wb.at[s], ad_sem.at[s, 2]))

        @pl.when(n >= 18)
        def _():
            rows = pl.ds(pl.multiple_of((n - 18) * 32, 32), 32)
            own = pl.ds(pl.multiple_of(me * 288 + (n - 18) * 32, 32), 32)
            act(pltpu.make_async_copy(md.at[layer, rows, :], mbd.at[s], ad_sem.at[s, 0]))
            act(pltpu.make_async_copy(vd.at[layer, rows, :], vbd.at[s], ad_sem.at[s, 1]))
            act(pltpu.make_async_copy(wd.at[layer, own, :], wbd.at[s], ad_sem.at[s, 2]))

    def new_weight(w, m, v, g):
        m = 0.9 * m + 0.1 * g
        v = 0.95 * v + 0.05 * g * g
        step = m * lax.rsqrt(v + 1e-8) + 0.1 * w
        return (w - 0.02 * step).astype(BF16)

    def weights_of(n, act):
        s = n % 2

        @pl.when(n < STEPS)
        def _():
            cols = pl.ds(pl.multiple_of(n * CF, CF), CF)
            act(pltpu.make_async_copy(wg.at[1, :, cols], wgj.at[s], w_sem.at[s, 0]))
            act(pltpu.make_async_copy(wu.at[1, :, cols], wuj.at[s], w_sem.at[s, 1]))
            act(pltpu.make_async_copy(wd.at[1, cols, :], wdj.at[s], w_sem.at[s, 2]))

        @pl.when((n >= STEPS) & (n < 2 * STEPS))
        def _():
            cols = pl.ds(pl.multiple_of((n - STEPS) * CF, CF), CF)
            act(pltpu.make_async_copy(wd.at[0, cols, :], wdj.at[s], w_sem.at[s, 2]))

    def saved_of(n, act):
        @pl.when((n >= STEPS) & (n < 2 * STEPS))
        def _():
            act(pltpu.make_async_copy(g0.at[n - STEPS], gbuf, gu_sem.at[0]))
            act(pltpu.make_async_copy(u0.at[n - STEPS], ubuf, gu_sem.at[1]))

    def keep_hidden(j):
        return pltpu.make_async_copy(hid_b, hid1_t.at[pl.ds(j * 8, 8)], hw_sem)

    def hidden_of(src, k, start):
        s = k % 2
        if start:
            for o in range(8):
                pltpu.make_async_copy(src.at[o * 9 + k], hid_c.at[s, o], hc_sem.at[s]).start()
        else:
            pltpu.make_async_copy(src.at[pl.ds(0, 8)], hid_c.at[s], hc_sem.at[s]).wait()

    whole = [
        pltpu.make_async_copy(dy, dyv, load_sem.at[0]),
        pltpu.make_async_copy(a1, av, load_sem.at[1]),
        pltpu.make_async_copy(a1_t, at, load_sem.at[2]),
    ]
    second_h = pltpu.make_async_copy(h1, av, load_sem.at[1])
    second_at = pltpu.make_async_copy(a0_t, at, load_sem.at[2])

    start = lambda copy: copy.start()
    wait = lambda copy: copy.wait()

    def grad_columns(q, d):
        @pl.loop(0, 2)
        def _(half):
            rows = pl.ds(pl.multiple_of(half * 448, 448), 448)
            out = nn(at[rows, :], d[...]).astype(BF16)
            for o in range(4):
                for h in range(2):
                    grad[q % RING, o % 2, half * 2 + o // 2, h * 112 : (h + 1) * 112, :] = out[
                        o * 112 : (o + 1) * 112, h * 128 : (h + 1) * 128
                    ]

    def grad_rows(q, k, d):
        out = nn(hid_c[k % 2].reshape(256, T), d[...]).astype(BF16)
        for o in range(8):
            for h in range(7):
                grad[q % RING, o % 2, o // 2, h * 32 : (h + 1) * 32, :] = out[
                    o * 32 : (o + 1) * 32, h * 128 : (h + 1) * 128
                ]

    def hidden_back(g, u, dp):
        s = sigmoid(g)
        act = g * s
        return act, (dp * u * (s + act * (1.0 - s))).astype(BF16), (dp * act).astype(BF16)

    def compute(s):
        @pl.when((s < 18) & (s % 2 == 0))
        def _():
            j = s // 2
            b = j % 2
            weights_of(j + 1, start)
            weights_of(j, wait)

            @pl.when(j == 0)
            def _():
                for copy in whole:
                    copy.wait()

            @pl.when(j > 0)
            def _():
                keep_hidden(j - 1).wait()

            @pl.loop(0, NRB)
            def _(r):
                rows = pl.ds(pl.multiple_of(r * RB, RB), RB)
                a = av[rows, :]
                g = nn(a, wgj[b])
                u = nn(a, wuj[b])
                dp = nt(dyv[rows, :], wdj[b]).astype(BF16).astype(F32)
                act, dgr, dur = hidden_back(g, u, dp)
                hid_b[:, :, rows] = (act * u).astype(BF16).T.reshape(8, 32, RB)
                dg[rows, :] = dgr
                du[rows, :] = dur

            keep_hidden(j).start()
            grad_columns(s, dg)

            @pl.when(j == STEPS - 1)
            def _():
                second_h.start()

        @pl.when((s < 18) & (s % 2 == 1))
        def _():
            j = s // 2
            b = j % 2
            grad_columns(s, du)

            @pl.loop(0, NRB)
            def _(r):
                rows = pl.ds(pl.multiple_of(r * RB, RB), RB)
                by_g = nt(dg[rows, :], wgj[b])
                by_u = nt(du[rows, :], wuj[b])

                @pl.when(j == 0)
                def _():
                    dag[rows, :] = by_g
                    dau[rows, :] = by_u

                @pl.when(j > 0)
                def _():
                    dag[rows, :] += by_g
                    dau[rows, :] += by_u

            @pl.when(j == STEPS - 1)
            def _():
                keep_hidden(j).wait()
                hidden_of(hid1_t, 0, True)
                second_at.start()
                second_h.wait()

                @pl.loop(0, T // 128)
                def _(r):
                    rows = pl.ds(pl.multiple_of(r * 128, 128), 128)
                    da = dag[rows, :].astype(BF16).astype(F32) + dau[rows, :].astype(BF16).astype(F32)
                    da = da.astype(BF16).astype(F32)
                    wide = av[rows, :].astype(F32)
                    scale = norm_scale(wide)
                    along = jnp.sum(da * wide, -1, keepdims=True) * (scale * scale * scale) * (-1.0 / D)
                    back = (da * scale + wide * along).astype(BF16)
                    av[rows, :] = (dyv[rows, :].astype(F32) + back.astype(F32)).astype(BF16)

        @pl.when((s >= 18) & (s < 27))
        def _():
            k = s - 18

            @pl.when(k < 8)
            def _():
                hidden_of(hid1_t, k + 1, True)

            hidden_of(hid1_t, k, False)
            grad_rows(s, k, dyv)

            @pl.when(k == 8)
            def _():
                second_at.wait()

        @pl.when((s >= 27) & (s < 45) & ((s - 27) % 2 == 0))
        def _():
            n = STEPS + (s - 27) // 2
            b = n % 2
            weights_of(n + 1, start)
            weights_of(n, wait)
            saved_of(n, wait)

            @pl.loop(0, NRB)
            def _(r):
                rows = pl.ds(pl.multiple_of(r * RB, RB), RB)
                dp = nt(av[rows, :], wdj[b]).astype(BF16).astype(F32)
                _, dgr, dur = hidden_back(gbuf[rows, :], ubuf[rows, :], dp)
                dg[rows, :] = dgr
                du[rows, :] = dur

            saved_of(n + 1, start)
            grad_columns(s, dg)

        @pl.when((s >= 27) & (s < 45) & ((s - 27) % 2 == 1))
        def _():
            grad_columns(s, du)

            @pl.when(s == 44)
            def _():
                hidden_of(hid0_t, 0, True)

        @pl.when((s >= 45) & (s < 54))
        def _():
            k = s - 45

            @pl.when(k < 8)
            def _():
                hidden_of(hid0_t, k + 1, True)

            hidden_of(hid0_t, k, False)
            grad_rows(s, k, av)

    f32 = lambda t: t.astype(F32)

    def exchange(s):
        q = s - 1

        @pl.when(valid(q))
        def _():
            to_partner(q).wait_recv()

        qr = s - 1 - 2 * z
        for zz in range(4):

            @pl.when(valid(qr) & (z == zz))
            def _():
                if zz > 0:
                    sum_right(qr, zz - 1).wait_recv()
                if zz < 3:

                    @pl.when(qr >= SENDS)
                    def _():
                        sum_right(qr - SENDS, zz).wait_send()

                    e = qr % RING
                    for to in range(zz + 1, 4):
                        t = f32(grad[e, c, to]) + f32(pin[e, to])
                        if zz > 0:
                            t = t + f32(rin[e, to])
                        rout[qr % SENDS, to] = t.astype(BF16)
                    sum_right(qr, zz).start()

        ql = s - 1 - 2 * (3 - z)
        for zz in range(4):

            @pl.when(valid(ql) & (z == zz))
            def _():
                if zz < 3:
                    sum_left(ql, zz + 1).wait_recv()
                if zz > 0:

                    @pl.when(ql >= SENDS)
                    def _():
                        sum_left(ql - SENDS, zz).wait_send()

                    e = ql % RING
                    for to in range(zz):
                        t = f32(grad[e, c, to]) + f32(pin[e, to])
                        if zz < 3:
                            t = t + f32(lin[e, to])
                        lout[ql % SENDS, to] = t.astype(BF16)
                    sum_left(ql, zz).start()

        for zz in range(4):

            @pl.when((qr >= Q) & (qr < Q + SENDS) & (z == zz))
            def _():
                if zz < 3:
                    sum_right(qr - SENDS, zz).wait_send()

            @pl.when((ql >= Q) & (ql < Q + SENDS) & (z == zz))
            def _():
                if zz > 0:
                    sum_left(ql - SENDS, zz).wait_send()

        @pl.when(valid(s - 6))
        def _():
            moments(s - 6, start)

        qf = s - 7

        @pl.when((qf >= SENDS) & (qf < Q + SENDS))
        def _():
            keep_grad(qf - SENDS).wait()

        @pl.when(valid(qf))
        def _():
            e, b = qf % RING, qf % SENDS
            gfin[...] = f32(grad[e, c, z]) + f32(pin[e, z])

            @pl.when(z > 0)
            def _():
                gfin[...] += f32(rin[e, z])

            @pl.when(z < 3)
            def _():
                gfin[...] += f32(lin[e, z])

            gownb[b] = gfin[...].astype(BF16)
            keep_grad(qf).start()
            moments(qf, wait)
            n = qf % PER_LAYER
            sl = qf % 2

            @pl.when(n < 18)
            def _():
                for h in range(2):
                    lanes = slice(h * 128, (h + 1) * 128)
                    part = slice(h * 112, (h + 1) * 112)
                    g = gownb[b, part, :].astype(F32)
                    wown[b, part, :] = new_weight(f32(wb[sl, :, lanes]), mb[sl, :, lanes], vb[sl, :, lanes], g)

            @pl.when(n >= 18)
            def _():
                for h in range(7):
                    lanes = slice(h * 128, (h + 1) * 128)
                    part = slice(h * 32, (h + 1) * 32)
                    g = gownb[b, part, :].astype(F32)
                    wown[b, part, :] = new_weight(f32(wbd[sl, :, lanes]), mbd[sl, :, lanes], vbd[sl, :, lanes], g)

            keep_new(qf).start()

        @pl.when(valid(s - 8))
        def _():
            keep_new(s - 8).wait()

        qar = s - 8 - 2 * z
        qal = s - 8 - 2 * (3 - z)
        for zz in range(4):

            @pl.when(valid(qar) & (z == zz))
            def _():
                if zz > 0:
                    new_right(qar, zz - 1).wait_recv()
                if zz < 3:

                    @pl.when(qar >= SENDS)
                    def _():
                        new_right(qar - SENDS, zz).wait_send()

                    new_right(qar, zz).start()

            @pl.when(valid(qal) & (z == zz))
            def _():
                if zz < 3:
                    new_left(qal, zz + 1).wait_recv()
                if zz > 0:

                    @pl.when(qal >= SENDS)
                    def _():
                        new_left(qal - SENDS, zz).wait_send()

                    new_left(qal, zz).start()

            @pl.when((qar >= Q) & (qar < Q + SENDS) & (z == zz))
            def _():
                if zz < 3:
                    new_right(qar - SENDS, zz).wait_send()

            @pl.when((qal >= Q) & (qal < Q + SENDS) & (z == zz))
            def _():
                if zz > 0:
                    new_left(qal - SENDS, zz).wait_send()

        qap = s - 14

        @pl.when((qap >= SENDS) & (qap < Q + SENDS))
        def _():
            new_partner(qap - SENDS, c).wait_send()

        @pl.when(valid(qap))
        def _():
            new_partner(qap, c).start()

        @pl.when(valid(s - 16))
        def _():
            new_partner(s - 16, 1 - c).wait_recv()

    for copy in whole:
        copy.start()
    weights_of(0, start)

    @pl.loop(0, LAST)
    def _(s):
        exchange(s)

        @pl.when(s < Q)
        def _():
            compute(s)

            @pl.when(s == 17)
            def _():
                saved_of(STEPS, start)

        @pl.when((s >= SENDS) & (s < Q + SENDS))
        def _():
            to_partner(s - SENDS).wait_send()

        @pl.when(s < Q)
        def _():
            to_partner(s).start()


def train(*operands):
    vm = pltpu.VMEM
    dma = pltpu.SemaphoreType.DMA
    any_ = pl.BlockSpec(memory_space=pl.ANY)
    return pl.pallas_call(
        train_kernel,
        in_specs=[any_] * len(operands),
        out_specs=[any_] * 3,
        out_shape=[
            jax.ShapeDtypeStruct((Q, 2, 4, ROWS, 128), BF16),
            jax.ShapeDtypeStruct((Q, ROWS, 128), BF16),
            jax.ShapeDtypeStruct((72, 32, T), BF16),
        ],
        scratch_shapes=[
            vm((T, D), BF16), vm((T, D), BF16), vm((D, T), BF16),
            vm((T, CF), F32), vm((T, CF), F32), vm((T, CF), BF16), vm((T, CF), BF16),
            vm((2, D, CF), BF16), vm((2, D, CF), BF16), vm((2, CF, D), BF16),
            vm((8, 32, T), BF16), vm((2, 8, 32, T), BF16),
            vm((T, D), F32), vm((T, D), F32),
            vm((RING, 2, 4, ROWS, 128), BF16), vm((RING, 4, ROWS, 128), BF16),
            vm((RING, 4, ROWS, 128), BF16), vm((RING, 4, ROWS, 128), BF16),
            vm((SENDS, 4, ROWS, 128), BF16), vm((SENDS, 4, ROWS, 128), BF16),
            vm((SENDS, ROWS, 128), BF16), vm((SENDS, ROWS, 128), BF16), vm((ROWS, 128), F32),
            vm((2, 112, CF), F32), vm((2, 112, CF), F32), vm((2, 112, CF), BF16),
            vm((2, 32, D), F32), vm((2, 32, D), F32), vm((2, 32, D), BF16),
            dma((3,)), dma((2, 3)), dma((2,)), dma, dma((2,)),
            dma((SENDS,)), dma((RING,)), dma((SENDS,)), dma((RING,)), dma((SENDS,)), dma((RING,)),
            dma((SENDS,)), dma((RING,)), dma((SENDS,)), dma((RING,)), dma((SENDS,)), dma((RING,)),
            dma((SENDS,)), dma((SENDS,)), dma((2, 3)),
        ],
        compiler_params=pltpu.CompilerParams(
            collective_id=0, has_side_effects=True, vmem_limit_bytes=VMEM_LIMIT
        ),
        name="train",
    )(*operands)


def finish_kernel(wt_g, wt_u, wt_d, gg, gu, gd, mg, mu, md, vg, vu, vd, owg, owu, owd, omg, omu, omd, ovg, ovu, ovd):
    for src, dst in ((wt_g, owg), (wt_u, owu)):
        for o in range(8):
            for h in range(2):
                dst[0, o * 112 : (o + 1) * 112, h * 128 : (h + 1) * 128] = src[0, o % 2, o // 2, h * 112 : (h + 1) * 112, :]
    for o in range(8):
        for h in range(7):
            owd[0, o, :, h * 128 : (h + 1) * 128] = wt_d[0, o % 2, o // 2, h * 32 : (h + 1) * 32, :]
    for g, m, v, om, ov, n, rows in ((gg, mg, vg, omg, ovg, 2, 112), (gu, mu, vu, omu, ovu, 2, 112), (gd, md, vd, omd, ovd, 7, 32)):
        for h in range(n):
            lanes = slice(h * 128, (h + 1) * 128)
            gr = g[0, h * rows : (h + 1) * rows, :].astype(F32)
            om[0, :, lanes] = 0.9 * m[0, :, lanes] + 0.1 * gr
            ov[0, :, lanes] = 0.95 * v[0, :, lanes] + 0.05 * gr * gr


def finish(wtmp, gown, m, v):
    layer = lambda i: i // STEPS
    first = lambda i: (1 - i // STEPS) * PER_LAYER
    chunk = (lambda i: first(i) + 2 * (i % STEPS), lambda i: first(i) + 2 * (i % STEPS) + 1, lambda i: first(i) + 18 + i % STEPS)
    blocks = [pl.BlockSpec((1, 2, 4, ROWS, 128), functools.partial(lambda f, i: (f(i), 0, 0, 0, 0), f)) for f in chunk]
    grads = [pl.BlockSpec((1, ROWS, 128), functools.partial(lambda f, i: (f(i), 0, 0), f)) for f in chunk]
    cols = pl.BlockSpec((1, 112, CF), lambda i: (layer(i), 0, i % STEPS))
    rows = pl.BlockSpec((1, 32, D), lambda i: (layer(i), i % STEPS, 0))
    wcols = pl.BlockSpec((1, D, CF), lambda i: (layer(i), 0, i % STEPS))
    wrows = pl.BlockSpec((1, 8, 32, D), lambda i: (layer(i), 0, i % STEPS, 0))
    out = pl.pallas_call(
        finish_kernel,
        grid=(2 * STEPS,),
        in_specs=[*blocks, *grads, cols, cols, rows, cols, cols, rows],
        out_specs=[wcols, wcols, wrows, cols, cols, rows, cols, cols, rows],
        out_shape=[
            jax.ShapeDtypeStruct((2, D, FF), BF16), jax.ShapeDtypeStruct((2, D, FF), BF16),
            jax.ShapeDtypeStruct((2, 8, 288, D), BF16),
            *[jax.ShapeDtypeStruct(t.shape, F32) for t in (*m, *v)],
        ],
        compiler_params=pltpu.CompilerParams(vmem_limit_bytes=VMEM_LIMIT, dimension_semantics=("arbitrary",)),
        name="finish",
    )(wtmp, wtmp, wtmp, gown, gown, gown, *m, *v)
    return (out[0], out[1], out[2].reshape(2, FF, D), *out[3:])


def solution(mesh):
    def step(x, dy, wg, wu, wd, *moments):
        m, v = moments[:3], moments[3:]
        g0, u0, hid0_t, a0_t, h1, a1, a1_t = forward(x[0], wg, wu, wd)
        wtmp, gown, _ = train(wg, wu, wd, *m, *v, dy[0], h1, a1, a1_t, a0_t, hid0_t, g0, u0)
        return finish(wtmp, gown, m, v)

    seq, whole, rows = P(("rep", "dp")), P(), P(None, "dp")
    return jax.shard_map(
        step, mesh=mesh,
        in_specs=(seq, seq, *[whole] * 3, *[rows] * 6),
        out_specs=(*[P("rep")] * 3, *[P("rep", "dp")] * 6),
        check_vma=False,
    )
```

time: 1020 us -> 464 us (0.45)
  waiting for transfers between devices: 643 us -> 0 us
  Pallas kernels: 0 us -> 462 us
  matrix products: 250 us -> 0 us
  other arithmetic: 64.5 us -> 0 us
  local copies, waits for them, and re-layouts: 40.7 us -> 0 us
  between operations: 15.2 us -> 0.65 us
    pallas_call x0 -> x3, Pallas kernels: none -> 462 us  [the longest x1 374 us: train(): pl.pallas_call(train_kernel, in_specs=[any_] * len(operands), out_specs=[...]
    unnamed x15 -> x0, waiting for transfers between devices: 406 us -> none
    dot_general x15 -> x0, matrix products: 250 us -> none  [the longest x5 91.6 us: layer(): up = jnp.dot(a, w['w_up'], preferred_element_type=jnp.float32)]
    reshape x3 -> x0, waiting for transfers between devices: 237 us -> none  [step(): t.reshape(-1, *t.shape[2:])]
    unnamed x35 -> x0, local copies, waits for them, and re-layouts: 40.1 us -> none
    unnamed x4 -> x0, other arithmetic: 37.3 us -> none
    reshape x3 -> x0, other arithmetic: 16.7 us -> none  [step(): t.reshape(-1, *t.shape[2:])]
  transfers between devices with their start and end apart: 9 -> 0, of which waited for: 8 -> 0; matrix products, arithmetic and copies ran while one was open for 14% -> 0% of each run, Pallas kernels for 0% -> 0%
where the time goes in v1:
time: 464 us; the launch traced here: 463 us
  Pallas kernels  462 us (100%)
    pallas_call x1, Pallas kernels, train(): pl.pallas_call(train_kernel, in_specs=[any_] * len(operands), out_specs=[...  374 us
    pallas_call x1, Pallas kernels, forward(): pl.pallas_call(forward_kernel, grid=(STEPS,), in_specs=[whole(T, D), pl.B...  57.1 us
    pallas_call x1, Pallas kernels, finish(): pl.pallas_call(finish_kernel, grid=(2 * STEPS,), in_specs=[*blocks, *grad...  31.2 us

profile of v1, /device:TPU:0, one launch (start us, length us, event | category | flops | bytes accessed | tf_op | source)
XLA Modules:
  0.0 463.0 jit_solution(9830365572601137528)
XLA Ops:
  0.6 57.1 %forward0.1 = (f32[9,2048,256]{2,1,0:T(8,128)}, f32[9,2048,256]{2,1,0:T(8,128)}, bf16[72,32,2048]{2,1,0:T(8,128)(2,1)}, bf16[896,2048]{1,0:T(8,128)(2,1)}, bf16[...) custom-call(bf16[2048,896]{1,0:T(8,128)(2,1)} %bitcast.3, bf16[2,896,2304]{2,1,0:T(8,128)(2,1)} %wg.3, ...), custom_call_target="tpu_custom_call" | custom-call | tf_op jit(solution)/shard_map/forward0/pallas_call | solution.py:92
  57.7 374.1 %train.1 = (bf16[54,2,4,224,128]{4,3,2,1,0:T(8,128)(2,1)}, bf16[54,224,128]{2,1,0:T(8,128)(2,1)}, bf16[72,32,2048]{2,1,0:T(8,128)(2,1)}) custom-call(bf16[2,896,2304]{2,1,0:T(8,128)(2,1)} %wg.3, bf16[2,896,2304]{2,1,0:T(8,128)(2,1)} %wu.3, bf16[2,2304,896]{2,1,0:T(8,128)(2,1)} %wd.3, f32[2,112,2304]{2,1,0:T(8,128)} %mg.3, f32[2,112,2304]{2,1,0:T(8,128)} %mu.3, ...), custom_call_target="tpu_custom_call" | custom-call | tf_op jit(solution)/shard_map/train/pallas_call | solution.py:608
  431.8 31.2 %finish.1 = (bf16[2,896,2304]{2,1,0:T(8,128)(2,1)}, bf16[2,896,2304]{2,1,0:T(8,128)(2,1)}, bf16[2,8,288,896]{3,2,1,0:T(8,128)(2,1)}, f32[2,112,2304]{2,1,0:T(8,1...) custom-call(bf16[54,2,4,224,128]{4,3,2,1,0:T(8,128)(2,1)} %get-tuple, ...), custom_call_target="tpu_custom_call" | custom-call | tf_op jit(solution)/shard_map/finish/pallas_call | solution.py:667

commit v2 on v1

--- a/solution.py
+++ b/solution.py
@@ -39,87 +39,12 @@
     return 1.0 / (1.0 + jnp.exp(-g))
 
 
-def forward_kernel(x, wg, wu, wd, g_out, u_out, hid_t, a0_t, h1, a1, a1_t, acc, a0):
-    j = pl.program_id(0)
-
-    @pl.when(j == 0)
-    def _():
-        @pl.loop(0, NRB)
-        def _(r):
-            rows = pl.ds(pl.multiple_of(r * RB, RB), RB)
-            wide = x[rows, :].astype(F32)
-            a = (wide * norm_scale(wide)).astype(BF16)
-            a0[rows, :] = a
-            a0_t[:, rows] = a.T
-
-    @pl.loop(0, NRB)
-    def _(r):
-        rows = pl.ds(pl.multiple_of(r * RB, RB), RB)
-        a = a0[rows, :]
-        g = nn(a, wg[0])
-        u = nn(a, wu[0])
-        g_out[0, rows, :] = g
-        u_out[0, rows, :] = u
-        hid = (g * sigmoid(g) * u).astype(BF16)
-        hid_t[:, :, rows] = hid.T.reshape(8, 32, RB)
-        y = nn(hid, wd[0])
-
-        @pl.when(j == 0)
-        def _():
-            acc[rows, :] = y
-
-        @pl.when(j > 0)
-        def _():
-            acc[rows, :] += y
-
-    @pl.when(j == STEPS - 1)
-    def _():
-        @pl.loop(0, NRB)
-        def _(r):
-            rows = pl.ds(pl.multiple_of(r * RB, RB), RB)
-            y = acc[rows, :].astype(BF16).astype(F32)
-            h = (x[rows, :].astype(F32) + y).astype(BF16)
-            h1[rows, :] = h
-            wide = h.astype(F32)
-            a = (wide * norm_scale(wide)).astype(BF16)
-            a1[rows, :] = a
-            a1_t[:, rows] = a.T
-
-
-def forward(x, wg, wu, wd):
-    whole = lambda *shape: pl.BlockSpec(shape, lambda j: (0,) * len(shape), pipeline_mode=pl.Buffered(1))
-    step = lambda *shape: pl.BlockSpec(shape, lambda j: (j,) + (0,) * (len(shape) - 1))
-    return pl.pallas_call(
-        forward_kernel,
-        grid=(STEPS,),
-        in_specs=[
-            whole(T, D),
-            pl.BlockSpec((1, D, CF), lambda j: (0, 0, j)),
-            pl.BlockSpec((1, D, CF), lambda j: (0, 0, j)),
-            pl.BlockSpec((1, CF, D), lambda j: (0, j, 0)),
-        ],
-        out_specs=[step(1, T, CF), step(1, T, CF), step(8, 32, T), whole(D, T), whole(T, D), whole(T, D), whole(D, T)],
-        out_shape=[
-            jax.ShapeDtypeStruct((STEPS, T, CF), F32),
-            jax.ShapeDtypeStruct((STEPS, T, CF), F32),
-            jax.ShapeDtypeStruct((72, 32, T), BF16),
-            jax.ShapeDtypeStruct((D, T), BF16),
-            jax.ShapeDtypeStruct((T, D), BF16),
-            jax.ShapeDtypeStruct((T, D), BF16),
-            jax.ShapeDtypeStruct((D, T), BF16),
-        ],
-        scratch_shapes=[pltpu.VMEM((T, D), F32), pltpu.VMEM((T, D), BF16)],
-        compiler_params=pltpu.CompilerParams(vmem_limit_bytes=VMEM_LIMIT, dimension_semantics=("arbitrary",)),
-        name="forward0",
-    )(x, wg, wu, wd)
-
-
 def train_kernel(
-    wg, wu, wd, mg, mu, md, vg, vu, vd, dy, h1, a1, a1_t, a0_t, hid0_t, g0, u0,
-    wtmp, gown, hid1_t,
-    dyv, av, at, gbuf, ubuf, dg, du, wgj, wuj, wdj, hid_b, hid_c, dag, dau,
+    wg, wu, wd, mg, mu, md, vg, vu, vd, x, dy,
+    wtmp, gown, hid0_t, hid1_t, a0_t, g0, u0, dg1, du1,
+    xv, dyv, av, at, gbuf, ubuf, dg, du, wgj, wuj, wdj, hid_b, hid_c,
     grad, pin, rin, lin, rout, lout, wown, gownb, gfin, mb, vb, wb, mbd, vbd, wbd,
-    load_sem, w_sem, gu_sem, hw_sem, hc_sem,
+    load_sem, w_sem, gu_sem, keep_sem, hw_sem, hc_sem, d_sem, da_sem,
     p_send, p_recv, r_send, r_recv, l_send, l_recv,
     ar_send, ar_recv, al_send, al_recv, ap_send, ap_recv, wo_sem, go_sem, ad_sem,
 ):
@@ -216,27 +141,43 @@
 
     def weights_of(n, act):
         s = n % 2
-
-        @pl.when(n < STEPS)
-        def _():
-            cols = pl.ds(pl.multiple_of(n * CF, CF), CF)
-            act(pltpu.make_async_copy(wg.at[1, :, cols], wgj.at[s], w_sem.at[s, 0]))
-            act(pltpu.make_async_copy(wu.at[1, :, cols], wuj.at[s], w_sem.at[s, 1]))
-            act(pltpu.make_async_copy(wd.at[1, cols, :], wdj.at[s], w_sem.at[s, 2]))
-
-        @pl.when((n >= STEPS) & (n < 2 * STEPS))
-        def _():
-            cols = pl.ds(pl.multiple_of((n - STEPS) * CF, CF), CF)
-            act(pltpu.make_async_copy(wd.at[0, cols, :], wdj.at[s], w_sem.at[s, 2]))
-
-    def saved_of(n, act):
-        @pl.when((n >= STEPS) & (n < 2 * STEPS))
-        def _():
-            act(pltpu.make_async_copy(g0.at[n - STEPS], gbuf, gu_sem.at[0]))
-            act(pltpu.make_async_copy(u0.at[n - STEPS], ubuf, gu_sem.at[1]))
+        cols = pl.ds(pl.multiple_of((n % STEPS) * CF, CF), CF)
+        layer = jnp.where((n >= STEPS) & (n < 2 * STEPS), 1, 0)
+
+        @pl.when(n < 2 * STEPS)
+        def _():
+            act(pltpu.make_async_copy(wg.at[layer, :, cols], wgj.at[s], w_sem.at[s, 0]))
+            act(pltpu.make_async_copy(wu.at[layer, :, cols], wuj.at[s], w_sem.at[s, 1]))
+
+        @pl.when(n < 3 * STEPS)
+        def _():
+            act(pltpu.make_async_copy(wd.at[layer, cols, :], wdj.at[s], w_sem.at[s, 2]))
+
+    def saved_of(j, act):
+        @pl.when(j < STEPS)
+        def _():
+            act(pltpu.make_async_copy(g0.at[j], gbuf, gu_sem.at[0]))
+            act(pltpu.make_async_copy(u0.at[j], ubuf, gu_sem.at[1]))
+
+    def keep_saved(j, r):
+        rows = pl.ds(pl.multiple_of(r * RB, RB), RB)
+        return (
+            pltpu.make_async_copy(gbuf.at[rows], g0.at[j, rows], keep_sem.at[r, 0]),
+            pltpu.make_async_copy(ubuf.at[rows], u0.at[j, rows], keep_sem.at[r, 1]),
+        )
+
+    def keep_hidden0(j):
+        return pltpu.make_async_copy(hid_c.at[j % 2], hid0_t.at[pl.ds(j * 8, 8)], hc_sem.at[j % 2])
 
     def keep_hidden(j):
         return pltpu.make_async_copy(hid_b, hid1_t.at[pl.ds(j * 8, 8)], hw_sem)
+
+    def keep_d(j):
+        cols = pl.ds(pl.multiple_of(j * CF, CF), CF)
+        return (
+            pltpu.make_async_copy(dg, dg1.at[:, cols], d_sem.at[0]),
+            pltpu.make_async_copy(du, du1.at[:, cols], d_sem.at[1]),
+        )
 
     def hidden_of(src, k, start):
         s = k % 2
@@ -246,27 +187,21 @@
         else:
             pltpu.make_async_copy(src.at[pl.ds(0, 8)], hid_c.at[s], hc_sem.at[s]).wait()
 
-    whole = [
-        pltpu.make_async_copy(dy, dyv, load_sem.at[0]),
-        pltpu.make_async_copy(a1, av, load_sem.at[1]),
-        pltpu.make_async_copy(a1_t, at, load_sem.at[2]),
-    ]
-    second_h = pltpu.make_async_copy(h1, av, load_sem.at[1])
-    second_at = pltpu.make_async_copy(a0_t, at, load_sem.at[2])
+    load_x = pltpu.make_async_copy(x, xv, load_sem.at[0])
+    load_dy = pltpu.make_async_copy(dy, dyv, load_sem.at[1])
+    keep_at = pltpu.make_async_copy(at, a0_t, load_sem.at[2])
+    load_at = pltpu.make_async_copy(a0_t, at, load_sem.at[2])
 
     start = lambda copy: copy.start()
     wait = lambda copy: copy.wait()
 
     def grad_columns(q, d):
-        @pl.loop(0, 2)
-        def _(half):
-            rows = pl.ds(pl.multiple_of(half * 448, 448), 448)
-            out = nn(at[rows, :], d[...]).astype(BF16)
-            for o in range(4):
-                for h in range(2):
-                    grad[q % RING, o % 2, half * 2 + o // 2, h * 112 : (h + 1) * 112, :] = out[
-                        o * 112 : (o + 1) * 112, h * 128 : (h + 1) * 128
-                    ]
+        out = nn(at[...], d[...]).astype(BF16)
+        for o in range(8):
+            for h in range(2):
+                grad[q % RING, o % 2, o // 2, h * 112 : (h + 1) * 112, :] = out[
+                    o * 112 : (o + 1) * 112, h * 128 : (h + 1) * 128
+                ]
 
     def grad_rows(q, k, d):
         out = nn(hid_c[k % 2].reshape(256, T), d[...]).astype(BF16)
@@ -281,26 +216,94 @@
         act = g * s
         return act, (dp * u * (s + act * (1.0 - s))).astype(BF16), (dp * act).astype(BF16)
 
-    def compute(s):
-        @pl.when((s < 18) & (s % 2 == 0))
-        def _():
-            j = s // 2
+    def rows_of(r, n=RB):
+        return pl.ds(pl.multiple_of(r * n, n), n)
+
+    def forward(acc):
+        weights_of(0, start)
+        load_x.start()
+        load_dy.start()
+        load_x.wait()
+
+        @pl.loop(0, NRB)
+        def _(r):
+            rows = rows_of(r)
+            wide = xv[rows, :].astype(F32)
+            a = (wide * norm_scale(wide)).astype(BF16)
+            av[rows, :] = a
+            at[:, rows] = a.T
+            acc[rows, :] = jnp.zeros((RB, D), F32)
+
+        keep_at.start()
+
+        @pl.loop(0, STEPS)
+        def _(j):
             b = j % 2
             weights_of(j + 1, start)
             weights_of(j, wait)
 
-            @pl.when(j == 0)
-            def _():
-                for copy in whole:
-                    copy.wait()
-
-            @pl.when(j > 0)
-            def _():
-                keep_hidden(j - 1).wait()
+            @pl.when(j > 1)
+            def _():
+                keep_hidden0(j - 2).wait()
 
             @pl.loop(0, NRB)
             def _(r):
-                rows = pl.ds(pl.multiple_of(r * RB, RB), RB)
+                rows = rows_of(r)
+
+                @pl.when(j > 0)
+                def _():
+                    for copy in keep_saved(j - 1, r):
+                        copy.wait()
+
+                a = av[rows, :]
+                g = nn(a, wgj[b])
+                u = nn(a, wuj[b])
+                gbuf[rows, :] = g
+                ubuf[rows, :] = u
+                hid = (g * sigmoid(g) * u).astype(BF16)
+                hid_c[b, :, :, rows] = hid.T.reshape(8, 32, RB)
+                acc[rows, :] += nn(hid, wdj[b])
+                for copy in keep_saved(j, r):
+                    copy.start()
+
+            keep_hidden0(j).start()
+
+        keep_at.wait()
+
+        @pl.loop(0, NRB)
+        def _(r):
+            rows = rows_of(r)
+            y = acc[rows, :].astype(BF16).astype(F32)
+            h = (xv[rows, :].astype(F32) + y).astype(BF16)
+            xv[rows, :] = h
+            wide = h.astype(F32)
+            a = (wide * norm_scale(wide)).astype(BF16)
+            av[rows, :] = a
+            at[:, rows] = a.T
+            for copy in keep_saved(STEPS - 1, r):
+                copy.wait()
+
+        keep_hidden0(STEPS - 2).wait()
+        keep_hidden0(STEPS - 1).wait()
+        load_dy.wait()
+
+    def first_layer(s):
+        @pl.when(s % 2 == 0)
+        def _():
+            j = s // 2
+            b = (j + 1) % 2
+            weights_of(STEPS + j + 1, start)
+            weights_of(STEPS + j, wait)
+
+            @pl.when(j > 0)
+            def _():
+                keep_hidden(j - 1).wait()
+                for copy in keep_d(j - 1):
+                    copy.wait()
+
+            @pl.loop(0, NRB)
+            def _(r):
+                rows = rows_of(r)
                 a = av[rows, :]
                 g = nn(a, wgj[b])
                 u = nn(a, wuj[b])
@@ -311,87 +314,96 @@
                 du[rows, :] = dur
 
             keep_hidden(j).start()
+            for copy in keep_d(j):
+                copy.start()
             grad_columns(s, dg)
 
-            @pl.when(j == STEPS - 1)
-            def _():
-                second_h.start()
-
-        @pl.when((s < 18) & (s % 2 == 1))
-        def _():
-            j = s // 2
+        @pl.when(s % 2 == 1)
+        def _():
+            grad_columns(s, du)
+
+            @pl.when(s == 17)
+            def _():
+                keep_hidden(STEPS - 1).wait()
+                for copy in keep_d(STEPS - 1):
+                    copy.wait()
+                hidden_of(hid1_t, 0, True)
+                load_at.start()
+                saved_of(0, start)
+
+    def between(s, wgl, wul, dgb, dub):
+        k = s - 18
+        block = lambda i: (
+            pltpu.make_async_copy(dg1.at[rows_of(i, 256)], dgb, da_sem.at[2]),
+            pltpu.make_async_copy(du1.at[rows_of(i, 256)], dub, da_sem.at[3]),
+        )
+        weights = (
+            pltpu.make_async_copy(wg.at[1], wgl, da_sem.at[0]),
+            pltpu.make_async_copy(wu.at[1], wul, da_sem.at[1]),
+        )
+
+        @pl.when(k == 0)
+        def _():
+            for copy in (*weights, *block(0)):
+                copy.start()
+
+        @pl.when(k < 8)
+        def _():
+            hidden_of(hid1_t, k + 1, True)
+
+        hidden_of(hid1_t, k, False)
+        grad_rows(s, k, dyv)
+
+        @pl.when(k == 1)
+        def _():
+            for copy in weights:
+                copy.wait()
+
+        @pl.when(k > 0)
+        def _():
+            for copy in block(k - 1):
+                copy.wait()
+            by_g = nt(dgb[...], wgl[...])
+            by_u = nt(dub[...], wul[...])
+            da = by_g.astype(BF16).astype(F32) + by_u.astype(BF16).astype(F32)
+            da = da.astype(BF16).astype(F32)
+            rows = rows_of(k - 1, 256)
+            wide = xv[rows, :].astype(F32)
+            scale = norm_scale(wide)
+            along = jnp.sum(da * wide, -1, keepdims=True) * (scale * scale * scale) * (-1.0 / D)
+            back = (da * scale + wide * along).astype(BF16)
+            xv[rows, :] = (dyv[rows, :].astype(F32) + back.astype(F32)).astype(BF16)
+
+            @pl.when(k < 8)
+            def _():
+                for copy in block(k):
+                    copy.start()
+
+        @pl.when(k == 8)
+        def _():
+            load_at.wait()
+
+    def last_layer(s):
+        @pl.when((s < 45) & ((s - 27) % 2 == 0))
+        def _():
+            j = (s - 27) // 2
             b = j % 2
-            grad_columns(s, du)
+            weights_of(2 * STEPS + j + 1, start)
+            weights_of(2 * STEPS + j, wait)
+            saved_of(j, wait)
 
             @pl.loop(0, NRB)
             def _(r):
-                rows = pl.ds(pl.multiple_of(r * RB, RB), RB)
-                by_g = nt(dg[rows, :], wgj[b])
-                by_u = nt(du[rows, :], wuj[b])
-
-                @pl.when(j == 0)
-                def _():
-                    dag[rows, :] = by_g
-                    dau[rows, :] = by_u
-
-                @pl.when(j > 0)
-                def _():
-                    dag[rows, :] += by_g
-                    dau[rows, :] += by_u
-
-            @pl.when(j == STEPS - 1)
-            def _():
-                keep_hidden(j).wait()
-                hidden_of(hid1_t, 0, True)
-                second_at.start()
-                second_h.wait()
-
-                @pl.loop(0, T // 128)
-                def _(r):
-                    rows = pl.ds(pl.multiple_of(r * 128, 128), 128)
-                    da = dag[rows, :].astype(BF16).astype(F32) + dau[rows, :].astype(BF16).astype(F32)
-                    da = da.astype(BF16).astype(F32)
-                    wide = av[rows, :].astype(F32)
-                    scale = norm_scale(wide)
-                    along = jnp.sum(da * wide, -1, keepdims=True) * (scale * scale * scale) * (-1.0 / D)
-                    back = (da * scale + wide * along).astype(BF16)
-                    av[rows, :] = (dyv[rows, :].astype(F32) + back.astype(F32)).astype(BF16)
-
-        @pl.when((s >= 18) & (s < 27))
-        def _():
-            k = s - 18
-
-            @pl.when(k < 8)
-            def _():
-                hidden_of(hid1_t, k + 1, True)
-
-            hidden_of(hid1_t, k, False)
-            grad_rows(s, k, dyv)
-
-            @pl.when(k == 8)
-            def _():
-                second_at.wait()
-
-        @pl.when((s >= 27) & (s < 45) & ((s - 27) % 2 == 0))
-        def _():
-            n = STEPS + (s - 27) // 2
-            b = n % 2
-            weights_of(n + 1, start)
-            weights_of(n, wait)
-            saved_of(n, wait)
-
-            @pl.loop(0, NRB)
-            def _(r):
-                rows = pl.ds(pl.multiple_of(r * RB, RB), RB)
-                dp = nt(av[rows, :], wdj[b]).astype(BF16).astype(F32)
+                rows = rows_of(r)
+                dp = nt(xv[rows, :], wdj[b]).astype(BF16).astype(F32)
                 _, dgr, dur = hidden_back(gbuf[rows, :], ubuf[rows, :], dp)
                 dg[rows, :] = dgr
                 du[rows, :] = dur
 
-            saved_of(n + 1, start)
+            saved_of(j + 1, start)
             grad_columns(s, dg)
 
-        @pl.when((s >= 27) & (s < 45) & ((s - 27) % 2 == 1))
+        @pl.when((s < 45) & ((s - 27) % 2 == 1))
         def _():
             grad_columns(s, du)
 
@@ -408,7 +420,7 @@
                 hidden_of(hid0_t, k + 1, True)
 
             hidden_of(hid0_t, k, False)
-            grad_rows(s, k, av)
+            grad_rows(s, k, xv)
 
     f32 = lambda t: t.astype(F32)
 
@@ -576,57 +588,59 @@
         def _():
             new_partner(s - 16, 1 - c).wait_recv()
 
-    for copy in whole:
-        copy.start()
-    weights_of(0, start)
-
-    @pl.loop(0, LAST)
-    def _(s):
-        exchange(s)
-
-        @pl.when(s < Q)
-        def _():
-            compute(s)
-
-            @pl.when(s == 17)
-            def _():
-                saved_of(STEPS, start)
-
-        @pl.when((s >= SENDS) & (s < Q + SENDS))
-        def _():
-            to_partner(s - SENDS).wait_send()
-
-        @pl.when(s < Q)
-        def _():
-            to_partner(s).start()
+    def slots(first, last, compute):
+        @pl.loop(first, last)
+        def _(s):
+            @pl.when(s < Q)
+            def _():
+                compute(s)
+
+            @pl.when((s >= SENDS) & (s < Q + SENDS))
+            def _():
+                to_partner(s - SENDS).wait_send()
+
+            @pl.when(s < Q)
+            def _():
+                to_partner(s).start()
+
+            exchange(s)
+
+    pl.run_scoped(forward, pltpu.VMEM((T, D), F32))
+    slots(0, 18, first_layer)
+    pl.run_scoped(
+        lambda *bufs: slots(18, 27, lambda s: between(s, *bufs)),
+        pltpu.VMEM((D, FF), BF16), pltpu.VMEM((D, FF), BF16), pltpu.VMEM((256, FF), BF16), pltpu.VMEM((256, FF), BF16),
+    )
+    slots(27, LAST, last_layer)
 
 
 def train(*operands):
     vm = pltpu.VMEM
     dma = pltpu.SemaphoreType.DMA
     any_ = pl.BlockSpec(memory_space=pl.ANY)
+    shape = jax.ShapeDtypeStruct
+    out_shape = [
+        shape((Q, 2, 4, ROWS, 128), BF16), shape((Q, ROWS, 128), BF16),
+        shape((72, 32, T), BF16), shape((72, 32, T), BF16), shape((D, T), BF16),
+        shape((STEPS, T, CF), F32), shape((STEPS, T, CF), F32), shape((T, FF), BF16), shape((T, FF), BF16),
+    ]
     return pl.pallas_call(
         train_kernel,
         in_specs=[any_] * len(operands),
-        out_specs=[any_] * 3,
-        out_shape=[
-            jax.ShapeDtypeStruct((Q, 2, 4, ROWS, 128), BF16),
-            jax.ShapeDtypeStruct((Q, ROWS, 128), BF16),
-            jax.ShapeDtypeStruct((72, 32, T), BF16),
-        ],
+        out_specs=[any_] * len(out_shape),
+        out_shape=out_shape,
         scratch_shapes=[
-            vm((T, D), BF16), vm((T, D), BF16), vm((D, T), BF16),
+            vm((T, D), BF16), vm((T, D), BF16), vm((T, D), BF16), vm((D, T), BF16),
             vm((T, CF), F32), vm((T, CF), F32), vm((T, CF), BF16), vm((T, CF), BF16),
             vm((2, D, CF), BF16), vm((2, D, CF), BF16), vm((2, CF, D), BF16),
             vm((8, 32, T), BF16), vm((2, 8, 32, T), BF16),
-            vm((T, D), F32), vm((T, D), F32),
             vm((RING, 2, 4, ROWS, 128), BF16), vm((RING, 4, ROWS, 128), BF16),
             vm((RING, 4, ROWS, 128), BF16), vm((RING, 4, ROWS, 128), BF16),
             vm((SENDS, 4, ROWS, 128), BF16), vm((SENDS, 4, ROWS, 128), BF16),
             vm((SENDS, ROWS, 128), BF16), vm((SENDS, ROWS, 128), BF16), vm((ROWS, 128), F32),
             vm((2, 112, CF), F32), vm((2, 112, CF), F32), vm((2, 112, CF), BF16),
             vm((2, 32, D), F32), vm((2, 32, D), F32), vm((2, 32, D), BF16),
-            dma((3,)), dma((2, 3)), dma((2,)), dma, dma((2,)),
+            dma((3,)), dma((2, 3)), dma((2,)), dma((NRB, 2)), dma, dma((2,)), dma((2,)), dma((4,)),
             dma((SENDS,)), dma((RING,)), dma((SENDS,)), dma((RING,)), dma((SENDS,)), dma((RING,)),
             dma((SENDS,)), dma((RING,)), dma((SENDS,)), dma((RING,)), dma((SENDS,)), dma((RING,)),
             dma((SENDS,)), dma((SENDS,)), dma((2, 3)),
@@ -683,8 +697,7 @@
 def solution(mesh):
     def step(x, dy, wg, wu, wd, *moments):
         m, v = moments[:3], moments[3:]
-        g0, u0, hid0_t, a0_t, h1, a1, a1_t = forward(x[0], wg, wu, wd)
-        wtmp, gown, _ = train(wg, wu, wd, *m, *v, dy[0], h1, a1, a1_t, a0_t, hid0_t, g0, u0)
+        wtmp, gown, *_ = train(wg, wu, wd, *m, *v, x[0], dy[0])
         return finish(wtmp, gown, m, v)
 
     seq, whole, rows = P(("rep", "dp")), P(), P(None, "dp")

time: 464 us -> 392 us (0.84)
  Pallas kernels: 462 us -> 391 us
    pallas_call x1 -> x0, Pallas kernels: 57.1 us -> none  [forward(): pl.pallas_call(forward_kernel, grid=(STEPS,), in_specs=[whole(T, D), pl.B...]
    pallas_call x1, Pallas kernels: 374 us -> 360 us  [train(): pl.pallas_call(train_kernel, in_specs=[any_] * len(operands), out_specs=[...]
where the time goes in v2:
time: 392 us
  Pallas kernels  391 us (100%)
    pallas_call x1, Pallas kernels, train(): pl.pallas_call(train_kernel, in_specs=[any_] * len(operands), out_specs=[...  360 us
    pallas_call x1, Pallas kernels, finish(): pl.pallas_call(finish_kernel, grid=(2 * STEPS,), in_specs=[*blocks, *grad...  31.2 us

profile of v2, /device:TPU:0, one launch (start us, length us, event | category | flops | bytes accessed | tf_op | source)
XLA Modules:
  0.0 391.5 jit_solution(7659182456354328396)
XLA Ops:
  0.6 359.5 %train.1 = (bf16[54,2,4,224,128]{4,3,2,1,0:T(8,128)(2,1)}, bf16[54,224,128]{2,1,0:T(8,128)(2,1)}, bf16[72,32,2048]{2,1,0:T(8,128)(2,1)}, bf16[72,32,2048]{2,1,0:...) custom-call(bf16[2,896,2304]{2,1,0:T(8,128)(2,1)} %wg.1, ...), custom_call_target="tpu_custom_call" | custom-call | tf_op jit(solution)/shard_map/train/pallas_call | solution.py:627
  360.2 31.2 %finish.1 = (bf16[2,896,2304]{2,1,0:T(8,128)(2,1)}, bf16[2,896,2304]{2,1,0:T(8,128)(2,1)}, bf16[2,8,288,896]{3,2,1,0:T(8,128)(2,1)}, f32[2,112,2304]{2,1,0:T(8,1...) custom-call(bf16[54,2,4,224,128]{4,3,2,1,0:T(8,128)(2,1)} %get-tuple, ...), custom_call_target="tpu_custom_call" | custom-call | tf_op jit(solution)/shard_map/finish/pallas_call | solution.py:681

commit v3 on v0

v3 whole, which is shorter than its diff:
```python
import jax
import jax.numpy as jnp
from jax import lax
from jax.experimental import pallas as pl
from jax.experimental.pallas import tpu as pltpu
from jax.sharding import PartitionSpec as P

MESH = pl.DeviceIdType.MESH
F32, BF16 = jnp.float32, jnp.bfloat16
T, D, FF = 2048, 896, 2304
CF = 256
STEPS = FF // CF
RB = 1024
NRB = T // RB
ROWS = 112
PER_LAYER = 27
CHUNKS = 2 * PER_LAYER
Q = 2 * CHUNKS
LAG = 2
HELD = 8
RING = 2 * HELD
SENDS = 4
SPREAD = 4 + 6 * LAG
LAST = Q + SPREAD + 3
VMEM_LIMIT = 67043328


def nt(a, b):
    return lax.dot_general(a, b, (((1,), (1,)), ((), ())), preferred_element_type=F32)


def nn(a, b):
    return jnp.dot(a, b, preferred_element_type=F32)


def norm_scale(wide):
    return lax.rsqrt(jnp.mean(wide * wide, -1, keepdims=True) + 1e-6)


def sigmoid(g):
    return 1.0 / (1.0 + jnp.exp(-g))


def train_kernel(
    wg, wu, wd, mg, mu, md, vg, vu, vd, x, dy,
    wtmp, nmg, nmu, nmd, nvg, nvu, nvd, hid0_t, hid1_t, g0, u0, dg1, du1,
    xv, dyv, av, at, gbuf, ubuf, dg, du, wgj, wuj, wdj, hid_b, hid_c,
    grad, pin, rin, lin, rout, lout, news, gfin, mb, vb, wb, mbd, vbd, wbd,
    load_sem, w_sem, gu_sem, keep_sem, hw_sem, hc_sem, d_sem, da_sem,
    p_send, p_recv, r_send, r_recv, l_send, l_recv,
    or_send, or_recv, ol_send, ol_recv, ar_send, ar_recv, al_send, al_recv, ap_send, ap_recv, wo_sem, mo_sem, ad_sem,
):
    rep, me = lax.axis_index("rep"), lax.axis_index("dp")
    z, c = me // 2, me % 2
    partner = (rep, z * 2 + (1 - c))
    right = (rep, jnp.minimum(z + 1, 3) * 2 + c)
    left = (rep, jnp.maximum(z - 1, 0) * 2 + c)

    bar = pltpu.get_barrier_semaphore()
    pl.semaphore_signal(bar, inc=1, device_id=partner, device_id_type=MESH)

    @pl.when(z < 3)
    def _():
        pl.semaphore_signal(bar, inc=1, device_id=right, device_id_type=MESH)

    @pl.when(z > 0)
    def _():
        pl.semaphore_signal(bar, inc=1, device_id=left, device_id_type=MESH)

    valid = lambda q: (q >= 0) & (q < Q)

    def remote(src, dst, send, recv, to):
        return pltpu.make_async_remote_copy(
            src_ref=src, dst_ref=dst, send_sem=send, recv_sem=recv, device_id=to, device_id_type=MESH
        )

    def to_partner(p):
        e = p % HELD
        return remote(grad.at[e, 1 - c], pin.at[e], p_send.at[p % 2], p_recv.at[e], partner)

    def sum_right(q, frm):
        part = pl.ds(frm + 1, 3 - frm)
        return remote(rout.at[q % SENDS, part], rin.at[q % RING, part], r_send.at[q % SENDS], r_recv.at[q % RING], right)

    def sum_left(q, frm):
        part = pl.ds(0, frm)
        return remote(lout.at[q % SENDS, part], lin.at[q % RING, part], l_send.at[q % SENDS], l_recv.at[q % RING], left)

    def own_right(q, frm):
        here = news.at[q % RING, pl.ds(frm, 1)]
        return remote(here, here, or_send.at[q % SENDS], or_recv.at[q % RING], right)

    def own_left(q, frm):
        here = news.at[q % RING, pl.ds(frm, 1)]
        return remote(here, here, ol_send.at[q % SENDS], ol_recv.at[q % RING], left)

    def on_right(q, frm):
        here = news.at[q % RING, pl.ds(0, frm)]
        return remote(here, here, ar_send.at[q % SENDS], ar_recv.at[q % RING], right)

    def on_left(q, frm):
        here = news.at[q % RING, pl.ds(frm + 1, 3 - frm)]
        return remote(here, here, al_send.at[q % SENDS], al_recv.at[q % RING], left)

    def new_partner(q, core):
        return remote(
            news.at[q % RING], wtmp.at[q // 2, core, q % 2], ap_send.at[q % SENDS], ap_recv.at[q % RING], partner
        )

    def keep_new(q):
        return pltpu.make_async_copy(news.at[q % RING], wtmp.at[q // 2, c, q % 2], wo_sem.at[q % SENDS])

    def moments(q, act, new=False):
        p = q // 2
        layer = jnp.where(p < PER_LAYER, 1, 0)
        n = p % PER_LAYER
        s = q % 2
        cols = pl.ds(pl.multiple_of((n // 2) * CF + s * 128, 128), 128)
        for which, (m, v, w, nm, nv) in enumerate(((mg, vg, wg, nmg, nvg), (mu, vu, wu, nmu, nvu))):

            @pl.when((n < 18) & (n % 2 == which))
            def _():
                if new:
                    act(pltpu.make_async_copy(mb.at[s], nm.at[layer, :, cols], mo_sem.at[s, 0]))
                    act(pltpu.make_async_copy(vb.at[s], nv.at[layer, :, cols], mo_sem.at[s, 1]))
                else:
                    own = pl.ds(pl.multiple_of(me * 112, 16), 112)
                    act(pltpu.make_async_copy(m.at[layer, :, cols], mb.at[s], ad_sem.at[s, 0]))
                    act(pltpu.make_async_copy(v.at[layer, :, cols], vb.at[s], ad_sem.at[s, 1]))
                    act(pltpu.make_async_copy(w.at[layer, own, cols], wb.at[s], ad_sem.at[s, 2]))

        @pl.when(n >= 18)
        def _():
            rows = pl.ds(pl.multiple_of((n - 18) * 32 + s * 16, 16), 16)
            if new:
                act(pltpu.make_async_copy(mbd.at[s], nmd.at[layer, rows, :], mo_sem.at[s, 0]))
                act(pltpu.make_async_copy(vbd.at[s], nvd.at[layer, rows, :], mo_sem.at[s, 1]))
            else:
                own = pl.ds(pl.multiple_of(me * 288 + (n - 18) * 32 + s * 16, 16), 16)
                act(pltpu.make_async_copy(md.at[layer, rows, :], mbd.at[s], ad_sem.at[s, 0]))
                act(pltpu.make_async_copy(vd.at[layer, rows, :], vbd.at[s], ad_sem.at[s, 1]))
                act(pltpu.make_async_copy(wd.at[layer, own, :], wbd.at[s], ad_sem.at[s, 2]))

    def adamw(w, m, v, g):
        m = 0.9 * m + 0.1 * g
        v = 0.95 * v + 0.05 * g * g
        step = m * lax.rsqrt(v + 1e-8) + 0.1 * w
        return (w - 0.02 * step).astype(BF16), m, v

    def weights_of(n, act):
        s = n % 2
        cols = pl.ds(pl.multiple_of((n % STEPS) * CF, CF), CF)
        layer = jnp.where((n >= STEPS) & (n < 2 * STEPS), 1, 0)

        @pl.when(n < 2 * STEPS)
        def _():
            act(pltpu.make_async_copy(wg.at[layer, :, cols], wgj.at[s], w_sem.at[s, 0]))
            act(pltpu.make_async_copy(wu.at[layer, :, cols], wuj.at[s], w_sem.at[s, 1]))

        @pl.when(n < 3 * STEPS)
        def _():
            act(pltpu.make_async_copy(wd.at[layer, cols, :], wdj.at[s], w_sem.at[s, 2]))

    def saved_of(j, act):
        @pl.when(j < STEPS)
        def _():
            act(pltpu.make_async_copy(g0.at[j], gbuf, gu_sem.at[0]))
            act(pltpu.make_async_copy(u0.at[j], ubuf, gu_sem.at[1]))

    def keep_saved(j, r):
        rows = pl.ds(pl.multiple_of(r * RB, RB), RB)
        return (
            pltpu.make_async_copy(gbuf.at[rows], g0.at[j, rows], keep_sem.at[r, 0]),
            pltpu.make_async_copy(ubuf.at[rows], u0.at[j, rows], keep_sem.at[r, 1]),
        )

    def keep_hidden0(j):
        return pltpu.make_async_copy(hid_c.at[j % 2], hid0_t.at[pl.ds(j * 8, 8)], hc_sem.at[j % 2])

    def keep_hidden(j):
        return pltpu.make_async_copy(hid_b, hid1_t.at[pl.ds(j * 8, 8)], hw_sem)

    def keep_d(j):
        cols = pl.ds(pl.multiple_of(j * CF, CF), CF)
        return (
            pltpu.make_async_copy(dg, dg1.at[:, cols], d_sem.at[0]),
            pltpu.make_async_copy(du, du1.at[:, cols], d_sem.at[1]),
        )

    def hidden_of(src, k, start):
        s = k % 2
        if start:
            for o in range(8):
                pltpu.make_async_copy(src.at[o * 9 + k], hid_c.at[s, o], hc_sem.at[s]).start()
        else:
            pltpu.make_async_copy(src.at[pl.ds(0, 8)], hid_c.at[s], hc_sem.at[s]).wait()

    load_dy = pltpu.make_async_copy(dy, dyv, load_sem.at[2])

    start = lambda copy: copy.start()
    wait = lambda copy: copy.wait()

    def grad_columns(p, d):
        out = nn(at[...], d[...]).astype(BF16)
        for o in range(8):
            for h in range(2):
                grad[p % HELD, o % 2, h, o // 2] = out[o * 112 : (o + 1) * 112, h * 128 : (h + 1) * 128]

    def grad_rows(p, k, d):
        out = nn(hid_c[k % 2].reshape(256, T), d[...]).astype(BF16)
        for o in range(8):
            for h in range(2):
                for i in range(7):
                    grad[p % HELD, o % 2, h, o // 2, i * 16 : (i + 1) * 16, :] = out[
                        o * 32 + h * 16 : o * 32 + h * 16 + 16, i * 128 : (i + 1) * 128
                    ]

    def hidden_back(g, u, dp):
        s = sigmoid(g)
        act = g * s
        return act, (dp * u * (s + act * (1.0 - s))).astype(BF16), (dp * act).astype(BF16)

    def rows_of(r, n=RB):
        return pl.ds(pl.multiple_of(r * n, n), n)

    def forward(acc):
        weights_of(0, start)
        halves = [pltpu.make_async_copy(x.at[rows_of(r)], xv.at[rows_of(r)], load_sem.at[r]) for r in range(NRB)]
        for copy in halves:
            copy.start()
        load_dy.start()
        for r in range(NRB):
            halves[r].wait()
            rows = rows_of(r)
            wide = xv[rows, :].astype(F32)
            av[rows, :] = (wide * norm_scale(wide)).astype(BF16)

        @pl.loop(0, NRB * STEPS)
        def _(i):
            j, r = i // NRB, i % NRB
            b = j % 2
            rows = rows_of(r)

            @pl.when(r == 0)
            def _():
                weights_of(j + 1, start)
                weights_of(j, wait)

                @pl.when(j > 1)
                def _():
                    keep_hidden0(j - 2).wait()

            @pl.when(j > 0)
            def _():
                for copy in keep_saved(j - 1, r):
                    copy.wait()

            a = av[rows, :]
            g = nn(a, wgj[b])
            u = nn(a, wuj[b])
            gbuf[rows, :] = g
            ubuf[rows, :] = u
            hid = (g * sigmoid(g) * u).astype(BF16)
            hid_c[b, :, :, rows] = hid.T.reshape(8, 32, RB)
            acc[rows, :] = jnp.where(j == 0, 0.0, acc[rows, :]) + nn(hid, wdj[b])
            for copy in keep_saved(j, r):
                copy.start()

            @pl.when(r == NRB - 1)
            def _():
                keep_hidden0(j).start()

        @pl.loop(0, NRB)
        def _(r):
            rows = rows_of(r)
            y = acc[rows, :].astype(BF16).astype(F32)
            h = (xv[rows, :].astype(F32) + y).astype(BF16)
            xv[rows, :] = h
            wide = h.astype(F32)
            a = (wide * norm_scale(wide)).astype(BF16)
            av[rows, :] = a
            at[:, rows] = a.T
            for copy in keep_saved(STEPS - 1, r):
                copy.wait()

        keep_hidden0(STEPS - 2).wait()
        keep_hidden0(STEPS - 1).wait()
        load_dy.wait()

    def first_layer(t):
        j = t // 4
        b = (j + 1) % 2

        @pl.when(t % 4 == 0)
        def _():
            weights_of(STEPS + j + 1, start)
            weights_of(STEPS + j, wait)

            @pl.when(j > 0)
            def _():
                keep_hidden(j - 1).wait()
                for copy in keep_d(j - 1):
                    copy.wait()

        @pl.when(t % 4 < 2)
        def _():
            rows = rows_of(t % 4)
            a = av[rows, :]
            g = nn(a, wgj[b])
            u = nn(a, wuj[b])
            dp = nt(dyv[rows, :], wdj[b]).astype(BF16).astype(F32)
            act, dgr, dur = hidden_back(g, u, dp)
            hid_b[:, :, rows] = (act * u).astype(BF16).T.reshape(8, 32, RB)
            dg[rows, :] = dgr
            du[rows, :] = dur

        @pl.when(t % 4 == 2)
        def _():
            keep_hidden(j).start()
            for copy in keep_d(j):
                copy.start()
            grad_columns(2 * j, dg)

        @pl.when(t % 4 == 3)
        def _():
            grad_columns(2 * j + 1, du)

            @pl.when(j == STEPS - 1)
            def _():
                keep_hidden(STEPS - 1).wait()
                for copy in keep_d(STEPS - 1):
                    copy.wait()
                hidden_of(hid1_t, 0, True)
                saved_of(0, start)

    def between(t, wgl, wul, dgb, dub, xb):
        k = (t - 36) // 2
        block = lambda i: (
            pltpu.make_async_copy(dg1.at[rows_of(i, 256)], dgb, da_sem.at[2]),
            pltpu.make_async_copy(du1.at[rows_of(i, 256)], dub, da_sem.at[3]),
            pltpu.make_async_copy(x.at[rows_of(i, 256)], xb, da_sem.at[4]),
        )
        weights = (
            pltpu.make_async_copy(wg.at[1], wgl, da_sem.at[0]),
            pltpu.make_async_copy(wu.at[1], wul, da_sem.at[1]),
        )

        @pl.when(t == 36)
        def _():
            for copy in (*weights, *block(0)):
                copy.start()

        @pl.when(t == 38)
        def _():
            for copy in weights:
                copy.wait()

        @pl.when((k > 0) & (t % 2 == 0))
        def _():
            for copy in block(k - 1):
                copy.wait()
            by_g = nt(dgb[...], wgl[...])
            by_u = nt(dub[...], wul[...])
            da = by_g.astype(BF16).astype(F32) + by_u.astype(BF16).astype(F32)
            da = da.astype(BF16).astype(F32)
            rows = rows_of(k - 1, 256)
            wide = xv[rows, :].astype(F32)
            scale = norm_scale(wide)
            along = jnp.sum(da * wide, -1, keepdims=True) * (scale * scale * scale) * (-1.0 / D)
            back = (da * scale + wide * along).astype(BF16)
            xv[rows, :] = (dyv[rows, :].astype(F32) + back.astype(F32)).astype(BF16)
            wide = xb[...].astype(F32)
            at[:, rows] = (wide * norm_scale(wide)).astype(BF16).T

            @pl.when(k < 8)
            def _():
                for copy in block(k):
                    copy.start()

        @pl.when(t % 2 == 1)
        def _():
            @pl.when(k < 8)
            def _():
                hidden_of(hid1_t, k + 1, True)

            hidden_of(hid1_t, k, False)
            grad_rows(18 + k, k, dyv)

    def last_layer(t):
        j = (t - 54) // 4
        b = j % 2
        turn = (t - 54) % 4
        k = (t - 90) // 2

        @pl.when((t < 90) & (turn == 0))
        def _():
            weights_of(2 * STEPS + j + 1, start)
            weights_of(2 * STEPS + j, wait)
            saved_of(j, wait)

        @pl.when((t < 90) & (turn < 2))
        def _():
            rows = rows_of(turn)
            dp = nt(xv[rows, :], wdj[b]).astype(BF16).astype(F32)
            _, dgr, dur = hidden_back(gbuf[rows, :], ubuf[rows, :], dp)
            dg[rows, :] = dgr
            du[rows, :] = dur

        @pl.when((t < 90) & (turn == 2))
        def _():
            saved_of(j + 1, start)
            grad_columns(PER_LAYER + 2 * j, dg)

        @pl.when((t < 90) & (turn == 3))
        def _():
            grad_columns(PER_LAYER + 2 * j + 1, du)

            @pl.when(t == 89)
            def _():
                hidden_of(hid0_t, 0, True)

        @pl.when((t >= 90) & (t < Q) & (t % 2 == 1))
        def _():
            @pl.when(k < 8)
            def _():
                hidden_of(hid0_t, k + 1, True)

            hidden_of(hid0_t, k, False)
            grad_rows(PER_LAYER + 18 + k, k, xv)

    def chunk_after(t):
        n = t % 54
        pair = n < 36
        return (t < Q) & jnp.where(pair, n % 4 >= 2, n % 2 == 1), (t // 54) * PER_LAYER + jnp.where(
            pair, 2 * (n // 4) + n % 2, n // 2
        )

    f32 = lambda t: t.astype(F32)

    def sums(t):
        q = t - 3

        @pl.when(valid(q) & (q % 2 == 0))
        def _():
            to_partner(q // 2).wait_recv()

        qr = t - 3 - LAG * z
        ql = t - 3 - LAG * (3 - z)

        def own(q, to):
            e = (q // 2) % HELD
            return f32(grad[e, c, q % 2, to]) + f32(pin[e, q % 2, to])

        for zz in range(4):

            @pl.when(z == zz)
            def _():
                @pl.when(valid(qr))
                def _():
                    if zz > 0:
                        sum_right(qr, zz - 1).wait_recv()
                    if zz < 3:

                        @pl.when(qr >= SENDS)
                        def _():
                            sum_right(qr - SENDS, zz).wait_send()

                        for to in range(zz + 1, 4):
                            total = own(qr, to)
                            if zz > 0:
                                total = total + f32(rin[qr % RING, to])
                            rout[qr % SENDS, to] = total.astype(BF16)
                        sum_right(qr, zz).start()

                @pl.when(valid(ql))
                def _():
                    if zz < 3:
                        sum_left(ql, zz + 1).wait_recv()
                    if zz > 0:

                        @pl.when(ql >= SENDS)
                        def _():
                            sum_left(ql - SENDS, zz).wait_send()

                        for to in range(zz):
                            total = own(ql, to)
                            if zz < 3:
                                total = total + f32(lin[ql % RING, to])
                            lout[ql % SENDS, to] = total.astype(BF16)
                        sum_left(ql, zz).start()

    def optimizer(t):
        q = t - 3 - LAG * jnp.maximum(z, 3 - z)

        @pl.when((q >= 1) & (q <= Q))
        def _():
            moments(q - 1, wait, new=True)

        @pl.when(valid(q + 1))
        def _():
            moments(q + 1, start)

        @pl.when(valid(q))
        def _():
            e, h = (q // 2) % HELD, q % 2
            gfin[...] = f32(grad[e, c, h, z]) + f32(pin[e, h, z])

            @pl.when(z > 0)
            def _():
                gfin[...] += f32(rin[q % RING, z])

            @pl.when(z < 3)
            def _():
                gfin[...] += f32(lin[q % RING, z])

            moments(q, wait)
            n = (q // 2) % PER_LAYER

            @pl.when(n < 18)
            def _():
                g = f32(gfin[...].astype(BF16))
                news[q % RING, z], mb[h], vb[h] = adamw(f32(wb[h]), mb[h], vb[h], g)

            @pl.when(n >= 18)
            def _():
                for i in range(7):
                    lanes = slice(i * 128, (i + 1) * 128)
                    part = slice(i * 16, (i + 1) * 16)
                    g = f32(gfin[part, :].astype(BF16))
                    news[q % RING, z, part, :], mbd[h, :, lanes], vbd[h, :, lanes] = adamw(
                        f32(wbd[h, :, lanes]), mbd[h, :, lanes], vbd[h, :, lanes], g
                    )

            moments(q, start, new=True)

    def send(copy, q, frm):
        @pl.when(q >= SENDS)
        def _():
            copy(q - SENDS, frm).wait_send()

        copy(q, frm).start()

    def spread(t):
        for zz in range(4):

            @pl.when(z == zz)
            def _():
                q = t - 4 - LAG * max(zz, 3 - zz)

                @pl.when(valid(q))
                def _():
                    if zz < 3:
                        send(own_right, q, zz)
                    if zz > 0:
                        send(own_left, q, zz)

                if zz in (1, 2):
                    near, far = t - 4 - 4 * LAG, t - 4 - 5 * LAG
                    qr, ql = (near, far) if zz == 1 else (far, near)

                    @pl.when(valid(qr))
                    def _():
                        own_right(qr, zz - 1).wait_recv()
                        if zz == 2:
                            on_right(qr, 1).wait_recv()
                        send(on_right, qr, zz)

                    @pl.when(valid(ql))
                    def _():
                        own_left(ql, zz + 1).wait_recv()
                        if zz == 1:
                            on_left(ql, 2).wait_recv()
                        send(on_left, ql, zz)
                else:
                    q = t - SPREAD

                    @pl.when(valid(q))
                    def _():
                        if zz == 3:
                            own_right(q, 2).wait_recv()
                            on_right(q, 2).wait_recv()
                        else:
                            own_left(q, 1).wait_recv()
                            on_left(q, 1).wait_recv()

        q = t - SPREAD

        @pl.when(valid(q))
        def _():
            @pl.when(q >= SENDS)
            def _():
                new_partner(q - SENDS, c).wait_send()
                keep_new(q - SENDS).wait()

            new_partner(q, c).start()
            keep_new(q).start()

        @pl.when(valid(q - 2))
        def _():
            new_partner(q - 2, 1 - c).wait_recv()

    def last_waits():
        for i in range(2):
            to_partner(CHUNKS - 2 + i).wait_send()
        for i in range(SENDS):
            keep_new(Q - SENDS + i).wait()
            new_partner(Q - SENDS + i, c).wait_send()
        for zz in range(4):

            @pl.when(z == zz)
            def _():
                for q in range(Q - SENDS, Q):
                    if zz < 3:
                        sum_right(q, zz).wait_send()
                        own_right(q, zz).wait_send()
                    if zz > 0:
                        sum_left(q, zz).wait_send()
                        own_left(q, zz).wait_send()
                    if zz in (1, 2):
                        on_right(q, zz).wait_send()
                        on_left(q, zz).wait_send()

    def slots(first, last, compute):
        @pl.loop(first, last)
        def _(t):
            compute(t)
            ready, p = chunk_after(t)

            @pl.when(ready)
            def _():
                @pl.when(p >= 2)
                def _():
                    to_partner(p - 2).wait_send()

                to_partner(p).start()

            sums(t)
            optimizer(t)
            spread(t)

    pl.run_scoped(forward, pltpu.VMEM((T, D), F32))
    @pl.when((z == 0) | (z == 3))
    def _():
        pl.semaphore_wait(bar, 2)

    @pl.when((z > 0) & (z < 3))
    def _():
        pl.semaphore_wait(bar, 3)

    slots(0, 36, first_layer)
    pl.run_scoped(
        lambda *bufs: slots(36, 54, lambda t: between(t, *bufs)),
        pltpu.VMEM((D, FF), BF16), pltpu.VMEM((D, FF), BF16),
        pltpu.VMEM((256, FF), BF16), pltpu.VMEM((256, FF), BF16), pltpu.VMEM((256, D), BF16),
    )
    slots(54, LAST, last_layer)
    last_waits()


def train(*operands):
    vm = pltpu.VMEM
    dma = pltpu.SemaphoreType.DMA
    any_ = pl.BlockSpec(memory_space=pl.ANY)
    shape = jax.ShapeDtypeStruct
    out_shape = [
        shape((CHUNKS, 2, 2, 4, ROWS, 128), BF16), *[shape(t.shape, F32) for t in operands[3:9]],
        shape((72, 32, T), BF16), shape((72, 32, T), BF16),
        shape((STEPS, T, CF), F32), shape((STEPS, T, CF), F32), shape((T, FF), BF16), shape((T, FF), BF16),
    ]
    return pl.pallas_call(
        train_kernel,
        in_specs=[any_] * len(operands),
        out_specs=[any_] * len(out_shape),
        out_shape=out_shape,
        scratch_shapes=[
            vm((T, D), BF16), vm((T, D), BF16), vm((T, D), BF16), vm((D, T), BF16),
            vm((T, CF), F32), vm((T, CF), F32), vm((T, CF), BF16), vm((T, CF), BF16),
            vm((2, D, CF), BF16), vm((2, D, CF), BF16), vm((2, CF, D), BF16),
            vm((8, 32, T), BF16), vm((2, 8, 32, T), BF16),
            vm((HELD, 2, 2, 4, ROWS, 128), BF16), vm((HELD, 2, 4, ROWS, 128), BF16),
            vm((RING, 4, ROWS, 128), BF16), vm((RING, 4, ROWS, 128), BF16),
            vm((SENDS, 4, ROWS, 128), BF16), vm((SENDS, 4, ROWS, 128), BF16),
            vm((RING, 4, ROWS, 128), BF16), vm((ROWS, 128), F32),
            vm((2, 112, 128), F32), vm((2, 112, 128), F32), vm((2, 112, 128), BF16),
            vm((2, 16, D), F32), vm((2, 16, D), F32), vm((2, 16, D), BF16),
            dma((3,)), dma((2, 3)), dma((2,)), dma((NRB, 2)), dma, dma((2,)), dma((2,)), dma((5,)),
            dma((2,)), dma((HELD,)), dma((SENDS,)), dma((RING,)), dma((SENDS,)), dma((RING,)),
            dma((SENDS,)), dma((RING,)), dma((SENDS,)), dma((RING,)), dma((SENDS,)), dma((RING,)),
            dma((SENDS,)), dma((RING,)), dma((SENDS,)), dma((RING,)), dma((SENDS,)), dma((2, 2)), dma((2, 3)),
        ],
        compiler_params=pltpu.CompilerParams(
            collective_id=0, has_side_effects=True, vmem_limit_bytes=VMEM_LIMIT
        ),
        name="train",
    )(*operands)


AHEAD = 12


def finish_kernel(
    wt, mg, mu, md, vg, vu, vd, owg, owu, owd, omg, omu, omd, ovg, ovu, ovd,
    wv, mgv, muv, mdv, vgv, vuv, vdv, columns, rows, w_sem, in_sem, out_sem, col_sem, row_sem,
):
    moments = ((mg, mgv, omg), (mu, muv, omu), (md, mdv, omd), (vg, vgv, ovg), (vu, vuv, ovu), (vd, vdv, ovd))
    pieces = [(i, layer) for layer in (1, 0) for i in range(6)]

    def take(i, layer):
        return pltpu.make_async_copy(moments[i][0].at[layer], moments[i][1].at[layer], in_sem.at[i, layer])

    def give(i, layer):
        return pltpu.make_async_copy(moments[i][1].at[layer], moments[i][2].at[layer], out_sem.at[i, layer])

    def chunk(p):
        return pltpu.make_async_copy(wt.at[p], wv.at[p], w_sem.at[p])

    def columns_out(out, layer, j, b):
        return pltpu.make_async_copy(columns.at[b], out.at[layer, :, pl.ds(pl.multiple_of(j * CF, CF), CF)], col_sem.at[b])

    def rows_out(layer, k, b):
        return pltpu.make_async_copy(rows.at[b], owd.at[layer, :, pl.ds(pl.multiple_of(k * 32, 32), 32), :], row_sem.at[b])

    for p in range(AHEAD):
        chunk(p).start()
    for i in range(2):
        take(*pieces[i]).start()

    def chunk_in(p):
        @pl.when(p + AHEAD < CHUNKS)
        def _():
            chunk(p + AHEAD).start()

        chunk(p).wait()

    for part in range(18):
        layer, base, n0 = 1 - part // 9, part // 9 * PER_LAYER, part % 9 * 3

        @pl.loop(0, 3)
        def _(i):
            n = n0 + i
            p = base + n
            chunk_in(p)
            if n0 < 18:
                b = n % 4

                @pl.when((n >= 4) | (base > 0))
                def _():
                    columns_out(owg, layer, 0, b).wait()

                for o in range(8):
                    for h in range(2):
                        columns[b, o * 112 : (o + 1) * 112, h * 128 : (h + 1) * 128] = wv[p, o % 2, h, o // 2]

                @pl.when(n % 2 == 0)
                def _():
                    columns_out(owg, layer, n // 2, b).start()

                @pl.when(n % 2 == 1)
                def _():
                    columns_out(owu, layer, n // 2, b).start()
            else:
                k = n - 18
                b = k % 4

                @pl.when((k >= 4) | (base > 0))
                def _():
                    rows_out(layer, 0, b).wait()

                for o in range(8):
                    for h in range(2):
                        for c in range(7):
                            rows[b, o, h * 16 : (h + 1) * 16, c * 128 : (c + 1) * 128] = wv[
                                p, o % 2, h, o // 2, c * 16 : (c + 1) * 16, :
                            ]
                rows_out(layer, k, b).start()

        if part < 12:
            take(*pieces[part]).wait()
            give(*pieces[part]).start()
            if part + 2 < 12:
                take(*pieces[part + 2]).start()

    for b in range(4):
        columns_out(owg, 0, 0, b).wait()
        rows_out(0, 0, b).wait()
    for piece in pieces:
        give(*piece).wait()


def finish(wtmp, *moments):
    vm, dma = pltpu.VMEM, pltpu.SemaphoreType.DMA
    any_ = pl.BlockSpec(memory_space=pl.ANY)
    out = pl.pallas_call(
        finish_kernel,
        in_specs=[any_] * 7,
        out_specs=[any_] * 9,
        out_shape=[
            jax.ShapeDtypeStruct((2, D, FF), BF16), jax.ShapeDtypeStruct((2, D, FF), BF16),
            jax.ShapeDtypeStruct((2, 8, 288, D), BF16),
            *[jax.ShapeDtypeStruct(t.shape, F32) for t in moments],
        ],
        scratch_shapes=[
            vm(wtmp.shape, BF16), *[vm(t.shape, F32) for t in moments], vm((4, D, CF), BF16), vm((4, 8, 32, D), BF16),
            dma((CHUNKS,)), dma((6, 2)), dma((6, 2)), dma((4,)), dma((4,)),
        ],
        compiler_params=pltpu.CompilerParams(vmem_limit_bytes=VMEM_LIMIT),
        name="finish",
    )(wtmp, *moments)
    return (out[0], out[1], out[2].reshape(2, FF, D), *out[3:])


def solution(mesh):
    def step(x, dy, wg, wu, wd, *moments):
        out = train(wg, wu, wd, *moments, x[0], dy[0])
        return finish(*out[:7])

    seq, whole, rows = P(("rep", "dp")), P(), P(None, "dp")
    return jax.shard_map(
        step, mesh=mesh,
        in_specs=(seq, seq, *[whole] * 3, *[rows] * 6),
        out_specs=(*[P("rep")] * 3, *[P("rep", "dp")] * 6),
        check_vma=False,
    )
```

time: 1020 us -> 368 us (0.36)
  waiting for transfers between devices: 643 us -> 0 us
  Pallas kernels: 0 us -> 367 us
  matrix products: 250 us -> 0 us
  other arithmetic: 64.5 us -> 0 us
  local copies, waits for them, and re-layouts: 40.7 us -> 0 us
  between operations: 15.2 us -> 0.84 us
    unnamed x15 -> x0, waiting for transfers between devices: 406 us -> none
    pallas_call x0 -> x2, Pallas kernels: none -> 367 us  [the longest x1 341 us: train(): pl.pallas_call(train_kernel, in_specs=[any_] * len(operands), out_specs=[...]
    dot_general x15 -> x0, matrix products: 250 us -> none  [the longest x5 91.6 us: layer(): up = jnp.dot(a, w['w_up'], preferred_element_type=jnp.float32)]
    reshape x3 -> x0, waiting for transfers between devices: 237 us -> none  [step(): t.reshape(-1, *t.shape[2:])]
    unnamed x35 -> x0, local copies, waits for them, and re-layouts: 40.1 us -> none
    unnamed x4 -> x0, other arithmetic: 37.3 us -> none
    reshape x3 -> x0, other arithmetic: 16.7 us -> none  [step(): t.reshape(-1, *t.shape[2:])]
  transfers between devices with their start and end apart: 9 -> 0, of which waited for: 8 -> 0; matrix products, arithmetic and copies ran while one was open for 14% -> 0% of each run, Pallas kernels for 0% -> 0%
where the time goes in v3:
time: 368 us
  Pallas kernels  367 us (100%)
    pallas_call x1, Pallas kernels, train(): pl.pallas_call(train_kernel, in_specs=[any_] * len(operands), out_specs=[...  341 us
    pallas_call x1, Pallas kernels, finish(): pl.pallas_call(finish_kernel, in_specs=[any_] * 7, out_specs=[any_] * 9,...  25.9 us

profile of v3, /device:TPU:0, one launch (start us, length us, event | category | flops | bytes accessed | tf_op | source)
XLA Modules:
  0.0 367.7 jit_solution(10817499167374571164)
XLA Ops:
  0.6 341.0 %train.1 = (bf16[54,2,2,4,112,128]{5,4,3,2,1,0:T(8,128)(2,1)}, f32[2,112,2304]{2,1,0:T(8,128)}, f32[2,112,2304]{2,1,0:T(8,128)}, f32[2,288,896]{2,1,0:T(8,128)},...) custom-call(bf16[2,896,2304]{2,1,0:T(8,128)(2,1)} %wg.1, ...), custom_call_target="tpu_custom_call" | custom-call | tf_op jit(solution)/shard_map/train/pallas_call | solution.py:670
  341.7 25.9 %finish.1 = (bf16[2,896,2304]{2,1,0:T(8,128)(2,1)}, bf16[2,896,2304]{2,1,0:T(8,128)(2,1)}, bf16[2,8,288,896]{3,2,1,0:T(8,128)(2,1)}, f32[2,112,2304]{2,1,0:T(8,1...) custom-call(bf16[54,2,2,4,112,128]{5,4,3,2,1,0:T(8,128)(2,1)} %get-t, ...), custom_call_target="tpu_custom_call" | custom-call | tf_op jit(solution)/shard_map/finish/pallas_call | solution.py:793

commit v4 on v3

--- a/solution.py
+++ b/solution.py
@@ -12,6 +12,9 @@
 STEPS = FF // CF
 RB = 1024
 NRB = T // RB
+LANES = 128
+HALF = 16
+OWN = 32
 ROWS = 112
 PER_LAYER = 27
 CHUNKS = 2 * PER_LAYER
@@ -115,7 +118,7 @@
         layer = jnp.where(p < PER_LAYER, 1, 0)
         n = p % PER_LAYER
         s = q % 2
-        cols = pl.ds(pl.multiple_of((n // 2) * CF + s * 128, 128), 128)
+        cols = pl.ds(pl.multiple_of((n // 2) * CF + s * LANES, LANES), LANES)
         for which, (m, v, w, nm, nv) in enumerate(((mg, vg, wg, nmg, nvg), (mu, vu, wu, nmu, nvu))):
 
             @pl.when((n < 18) & (n % 2 == which))
@@ -124,19 +127,19 @@
                     act(pltpu.make_async_copy(mb.at[s], nm.at[layer, :, cols], mo_sem.at[s, 0]))
                     act(pltpu.make_async_copy(vb.at[s], nv.at[layer, :, cols], mo_sem.at[s, 1]))
                 else:
-                    own = pl.ds(pl.multiple_of(me * 112, 16), 112)
+                    own = pl.ds(pl.multiple_of(me * ROWS, HALF), ROWS)
                     act(pltpu.make_async_copy(m.at[layer, :, cols], mb.at[s], ad_sem.at[s, 0]))
                     act(pltpu.make_async_copy(v.at[layer, :, cols], vb.at[s], ad_sem.at[s, 1]))
                     act(pltpu.make_async_copy(w.at[layer, own, cols], wb.at[s], ad_sem.at[s, 2]))
 
         @pl.when(n >= 18)
         def _():
-            rows = pl.ds(pl.multiple_of((n - 18) * 32 + s * 16, 16), 16)
+            rows = pl.ds(pl.multiple_of((n - 18) * OWN + s * HALF, HALF), HALF)
             if new:
                 act(pltpu.make_async_copy(mbd.at[s], nmd.at[layer, rows, :], mo_sem.at[s, 0]))
                 act(pltpu.make_async_copy(vbd.at[s], nvd.at[layer, rows, :], mo_sem.at[s, 1]))
             else:
-                own = pl.ds(pl.multiple_of(me * 288 + (n - 18) * 32 + s * 16, 16), 16)
+                own = pl.ds(pl.multiple_of(me * 288 + (n - 18) * OWN + s * HALF, HALF), HALF)
                 act(pltpu.make_async_copy(md.at[layer, rows, :], mbd.at[s], ad_sem.at[s, 0]))
                 act(pltpu.make_async_copy(vd.at[layer, rows, :], vbd.at[s], ad_sem.at[s, 1]))
                 act(pltpu.make_async_copy(wd.at[layer, own, :], wbd.at[s], ad_sem.at[s, 2]))
@@ -201,18 +204,18 @@
     wait = lambda copy: copy.wait()
 
     def grad_columns(p, d):
-        out = nn(at[...], d[...]).astype(BF16)
+        out = nn(at[:], d[:]).astype(BF16)
         for o in range(8):
             for h in range(2):
-                grad[p % HELD, o % 2, h, o // 2] = out[o * 112 : (o + 1) * 112, h * 128 : (h + 1) * 128]
+                grad[p % HELD, o % 2, h, o // 2] = out[o * ROWS : (o + 1) * ROWS, h * LANES : (h + 1) * LANES]
 
     def grad_rows(p, k, d):
-        out = nn(hid_c[k % 2].reshape(256, T), d[...]).astype(BF16)
+        out = nn(hid_c[k % 2].reshape(CF, T), d[:]).astype(BF16)
         for o in range(8):
             for h in range(2):
                 for i in range(7):
-                    grad[p % HELD, o % 2, h, o // 2, i * 16 : (i + 1) * 16, :] = out[
-                        o * 32 + h * 16 : o * 32 + h * 16 + 16, i * 128 : (i + 1) * 128
+                    grad[p % HELD, o % 2, h, o // 2, i * HALF : (i + 1) * HALF, :] = out[
+                        o * OWN + h * HALF : o * OWN + h * HALF + HALF, i * LANES : (i + 1) * LANES
                     ]
 
     def hidden_back(g, u, dp):
@@ -229,14 +232,19 @@
         for copy in halves:
             copy.start()
         load_dy.start()
-        for r in range(NRB):
-            halves[r].wait()
+        def normed_input(r):
+            wide = xv[rows_of(r), :].astype(F32)
+            av[rows_of(r), :] = (wide * norm_scale(wide)).astype(BF16)
+
+        def output(r):
             rows = rows_of(r)
-            wide = xv[rows, :].astype(F32)
+            y = acc[rows, :].astype(BF16).astype(F32)
+            h = (xv[rows, :].astype(F32) + y).astype(BF16)
+            xv[rows, :] = h
+            wide = h.astype(F32)
             av[rows, :] = (wide * norm_scale(wide)).astype(BF16)
 
-        @pl.loop(0, NRB * STEPS)
-        def _(i):
+        def step(i, first, beside=None):
             j, r = i // NRB, i % NRB
             b = j % 2
             rows = rows_of(r)
@@ -261,8 +269,11 @@
             gbuf[rows, :] = g
             ubuf[rows, :] = u
             hid = (g * sigmoid(g) * u).astype(BF16)
-            hid_c[b, :, :, rows] = hid.T.reshape(8, 32, RB)
-            acc[rows, :] = jnp.where(j == 0, 0.0, acc[rows, :]) + nn(hid, wdj[b])
+            hid_c[b, :, :, rows] = hid.T.reshape(8, OWN, RB)
+            y = nn(hid, wdj[b])
+            acc[rows, :] = y if first else acc[rows, :] + y
+            if beside:
+                beside()
             for copy in keep_saved(j, r):
                 copy.start()
 
@@ -270,21 +281,18 @@
             def _():
                 keep_hidden0(j).start()
 
-        @pl.loop(0, NRB)
-        def _(r):
-            rows = rows_of(r)
-            y = acc[rows, :].astype(BF16).astype(F32)
-            h = (xv[rows, :].astype(F32) + y).astype(BF16)
-            xv[rows, :] = h
-            wide = h.astype(F32)
-            a = (wide * norm_scale(wide)).astype(BF16)
-            av[rows, :] = a
-            at[:, rows] = a.T
-            for copy in keep_saved(STEPS - 1, r):
-                copy.wait()
-
-        keep_hidden0(STEPS - 2).wait()
-        keep_hidden0(STEPS - 1).wait()
+        halves[0].wait()
+        normed_input(0)
+        halves[1].wait()
+        step(0, True, lambda: normed_input(1))
+        step(1, True)
+
+        @pl.loop(NRB, NRB * STEPS - 1)
+        def _(i):
+            step(i, False)
+
+        step(NRB * STEPS - 1, False, lambda: output(0))
+        output(1)
         load_dy.wait()
 
     def first_layer(t):
@@ -306,11 +314,12 @@
         def _():
             rows = rows_of(t % 4)
             a = av[rows, :]
+            at[:, rows] = a.T
             g = nn(a, wgj[b])
             u = nn(a, wuj[b])
             dp = nt(dyv[rows, :], wdj[b]).astype(BF16).astype(F32)
             act, dgr, dur = hidden_back(g, u, dp)
-            hid_b[:, :, rows] = (act * u).astype(BF16).T.reshape(8, 32, RB)
+            hid_b[:, :, rows] = (act * u).astype(BF16).T.reshape(8, OWN, RB)
             dg[rows, :] = dgr
             du[rows, :] = dur
 
@@ -330,15 +339,20 @@
                 keep_hidden(STEPS - 1).wait()
                 for copy in keep_d(STEPS - 1):
                     copy.wait()
+                for r in range(NRB):
+                    for copy in keep_saved(STEPS - 1, r):
+                        copy.wait()
+                for i in range(2):
+                    keep_hidden0(STEPS - 2 + i).wait()
                 hidden_of(hid1_t, 0, True)
                 saved_of(0, start)
 
     def between(t, wgl, wul, dgb, dub, xb):
         k = (t - 36) // 2
         block = lambda i: (
-            pltpu.make_async_copy(dg1.at[rows_of(i, 256)], dgb, da_sem.at[2]),
-            pltpu.make_async_copy(du1.at[rows_of(i, 256)], dub, da_sem.at[3]),
-            pltpu.make_async_copy(x.at[rows_of(i, 256)], xb, da_sem.at[4]),
+            pltpu.make_async_copy(dg1.at[rows_of(i, CF)], dgb, da_sem.at[2]),
+            pltpu.make_async_copy(du1.at[rows_of(i, CF)], dub, da_sem.at[3]),
+            pltpu.make_async_copy(x.at[rows_of(i, CF)], xb, da_sem.at[4]),
         )
         weights = (
             pltpu.make_async_copy(wg.at[1], wgl, da_sem.at[0]),
@@ -359,17 +373,17 @@
         def _():
             for copy in block(k - 1):
                 copy.wait()
-            by_g = nt(dgb[...], wgl[...])
-            by_u = nt(dub[...], wul[...])
+            by_g = nt(wgl[:], dgb[:])
+            by_u = nt(wul[:], dub[:])
             da = by_g.astype(BF16).astype(F32) + by_u.astype(BF16).astype(F32)
-            da = da.astype(BF16).astype(F32)
-            rows = rows_of(k - 1, 256)
+            da = da.astype(BF16).T.astype(F32)
+            rows = rows_of(k - 1, CF)
             wide = xv[rows, :].astype(F32)
             scale = norm_scale(wide)
             along = jnp.sum(da * wide, -1, keepdims=True) * (scale * scale * scale) * (-1.0 / D)
             back = (da * scale + wide * along).astype(BF16)
             xv[rows, :] = (dyv[rows, :].astype(F32) + back.astype(F32)).astype(BF16)
-            wide = xb[...].astype(F32)
+            wide = xb[:].astype(F32)
             at[:, rows] = (wide * norm_scale(wide)).astype(BF16).T
 
             @pl.when(k < 8)
@@ -503,29 +517,29 @@
         @pl.when(valid(q))
         def _():
             e, h = (q // 2) % HELD, q % 2
-            gfin[...] = f32(grad[e, c, h, z]) + f32(pin[e, h, z])
+            gfin[:] = f32(grad[e, c, h, z]) + f32(pin[e, h, z])
 
             @pl.when(z > 0)
             def _():
-                gfin[...] += f32(rin[q % RING, z])
+                gfin[:] += f32(rin[q % RING, z])
 
             @pl.when(z < 3)
             def _():
-                gfin[...] += f32(lin[q % RING, z])
+                gfin[:] += f32(lin[q % RING, z])
 
             moments(q, wait)
             n = (q // 2) % PER_LAYER
 
             @pl.when(n < 18)
             def _():
-                g = f32(gfin[...].astype(BF16))
+                g = f32(gfin[:].astype(BF16))
                 news[q % RING, z], mb[h], vb[h] = adamw(f32(wb[h]), mb[h], vb[h], g)
 
             @pl.when(n >= 18)
             def _():
                 for i in range(7):
-                    lanes = slice(i * 128, (i + 1) * 128)
-                    part = slice(i * 16, (i + 1) * 16)
+                    lanes = slice(i * LANES, (i + 1) * LANES)
+                    part = slice(i * HALF, (i + 1) * HALF)
                     g = f32(gfin[part, :].astype(BF16))
                     news[q % RING, z, part, :], mbd[h, :, lanes], vbd[h, :, lanes] = adamw(
                         f32(wbd[h, :, lanes]), mbd[h, :, lanes], vbd[h, :, lanes], g
@@ -651,7 +665,7 @@
     pl.run_scoped(
         lambda *bufs: slots(36, 54, lambda t: between(t, *bufs)),
         pltpu.VMEM((D, FF), BF16), pltpu.VMEM((D, FF), BF16),
-        pltpu.VMEM((256, FF), BF16), pltpu.VMEM((256, FF), BF16), pltpu.VMEM((256, D), BF16),
+        pltpu.VMEM((CF, FF), BF16), pltpu.VMEM((CF, FF), BF16), pltpu.VMEM((CF, D), BF16),
     )
     slots(54, LAST, last_layer)
     last_waits()
@@ -663,8 +677,8 @@
     any_ = pl.BlockSpec(memory_space=pl.ANY)
     shape = jax.ShapeDtypeStruct
     out_shape = [
-        shape((CHUNKS, 2, 2, 4, ROWS, 128), BF16), *[shape(t.shape, F32) for t in operands[3:9]],
-        shape((72, 32, T), BF16), shape((72, 32, T), BF16),
+        shape((CHUNKS, 2, 2, 4, ROWS, LANES), BF16), *[shape(t.shape, F32) for t in operands[3:9]],
+        shape((72, OWN, T), BF16), shape((72, OWN, T), BF16),
         shape((STEPS, T, CF), F32), shape((STEPS, T, CF), F32), shape((T, FF), BF16), shape((T, FF), BF16),
     ]
     return pl.pallas_call(
@@ -676,13 +690,13 @@
             vm((T, D), BF16), vm((T, D), BF16), vm((T, D), BF16), vm((D, T), BF16),
             vm((T, CF), F32), vm((T, CF), F32), vm((T, CF), BF16), vm((T, CF), BF16),
             vm((2, D, CF), BF16), vm((2, D, CF), BF16), vm((2, CF, D), BF16),
-            vm((8, 32, T), BF16), vm((2, 8, 32, T), BF16),
-            vm((HELD, 2, 2, 4, ROWS, 128), BF16), vm((HELD, 2, 4, ROWS, 128), BF16),
-            vm((RING, 4, ROWS, 128), BF16), vm((RING, 4, ROWS, 128), BF16),
-            vm((SENDS, 4, ROWS, 128), BF16), vm((SENDS, 4, ROWS, 128), BF16),
-            vm((RING, 4, ROWS, 128), BF16), vm((ROWS, 128), F32),
-            vm((2, 112, 128), F32), vm((2, 112, 128), F32), vm((2, 112, 128), BF16),
-            vm((2, 16, D), F32), vm((2, 16, D), F32), vm((2, 16, D), BF16),
+            vm((8, OWN, T), BF16), vm((2, 8, OWN, T), BF16),
+            vm((HELD, 2, 2, 4, ROWS, LANES), BF16), vm((HELD, 2, 4, ROWS, LANES), BF16),
+            vm((RING, 4, ROWS, LANES), BF16), vm((RING, 4, ROWS, LANES), BF16),
+            vm((SENDS, 4, ROWS, LANES), BF16), vm((SENDS, 4, ROWS, LANES), BF16),
+            vm((RING, 4, ROWS, LANES), BF16), vm((ROWS, LANES), F32),
+            vm((2, ROWS, LANES), F32), vm((2, ROWS, LANES), F32), vm((2, ROWS, LANES), BF16),
+            vm((2, HALF, D), F32), vm((2, HALF, D), F32), vm((2, HALF, D), BF16),
             dma((3,)), dma((2, 3)), dma((2,)), dma((NRB, 2)), dma, dma((2,)), dma((2,)), dma((5,)),
             dma((2,)), dma((HELD,)), dma((SENDS,)), dma((RING,)), dma((SENDS,)), dma((RING,)),
             dma((SENDS,)), dma((RING,)), dma((SENDS,)), dma((RING,)), dma((SENDS,)), dma((RING,)),
@@ -718,7 +732,7 @@
         return pltpu.make_async_copy(columns.at[b], out.at[layer, :, pl.ds(pl.multiple_of(j * CF, CF), CF)], col_sem.at[b])
 
     def rows_out(layer, k, b):
-        return pltpu.make_async_copy(rows.at[b], owd.at[layer, :, pl.ds(pl.multiple_of(k * 32, 32), 32), :], row_sem.at[b])
+        return pltpu.make_async_copy(rows.at[b], owd.at[layer, :, pl.ds(pl.multiple_of(k * OWN, OWN), OWN), :], row_sem.at[b])
 
     for p in range(AHEAD):
         chunk(p).start()
@@ -749,7 +763,7 @@
 
                 for o in range(8):
                     for h in range(2):
-                        columns[b, o * 112 : (o + 1) * 112, h * 128 : (h + 1) * 128] = wv[p, o % 2, h, o // 2]
+                        columns[b, o * ROWS : (o + 1) * ROWS, h * LANES : (h + 1) * LANES] = wv[p, o % 2, h, o // 2]
 
                 @pl.when(n % 2 == 0)
                 def _():
@@ -769,8 +783,8 @@
                 for o in range(8):
                     for h in range(2):
                         for c in range(7):
-                            rows[b, o, h * 16 : (h + 1) * 16, c * 128 : (c + 1) * 128] = wv[
-                                p, o % 2, h, o // 2, c * 16 : (c + 1) * 16, :
+                            rows[b, o, h * HALF : (h + 1) * HALF, c * LANES : (c + 1) * LANES] = wv[
+                                p, o % 2, h, o // 2, c * HALF : (c + 1) * HALF, :
                             ]
                 rows_out(layer, k, b).start()
 
@@ -800,7 +814,7 @@
             *[jax.ShapeDtypeStruct(t.shape, F32) for t in moments],
         ],
         scratch_shapes=[
-            vm(wtmp.shape, BF16), *[vm(t.shape, F32) for t in moments], vm((4, D, CF), BF16), vm((4, 8, 32, D), BF16),
+            vm(wtmp.shape, BF16), *[vm(t.shape, F32) for t in moments], vm((4, D, CF), BF16), vm((4, 8, OWN, D), BF16),
             dma((CHUNKS,)), dma((6, 2)), dma((6, 2)), dma((4,)), dma((4,)),
         ],
         compiler_params=pltpu.CompilerParams(vmem_limit_bytes=VMEM_LIMIT),

time: 368 us -> 364 us (0.989)
  Pallas kernels: 367 us -> 363 us
    pallas_call x1, Pallas kernels: 341 us -> 337 us  [train(): pl.pallas_call(train_kernel, in_specs=[any_] * len(operands), out_specs=[...]
where the time goes in v4:
time: 364 us
  Pallas kernels  363 us (100%)
    pallas_call x1, Pallas kernels, train(): pl.pallas_call(train_kernel, in_specs=[any_] * len(operands), out_specs=[...  337 us
    pallas_call x1, Pallas kernels, finish(): pl.pallas_call(finish_kernel, in_specs=[any_] * 7, out_specs=[any_] * 9,...  25.9 us

profile of v4, /device:TPU:0, one launch (start us, length us, event | category | flops | bytes accessed | tf_op | source)
XLA Modules:
  0.0 363.7 jit_solution(213475603388904043)
XLA Ops:
  0.6 337.0 %train.1 = (bf16[54,2,2,4,112,128]{5,4,3,2,1,0:T(8,128)(2,1)}, f32[2,112,2304]{2,1,0:T(8,128)}, f32[2,112,2304]{2,1,0:T(8,128)}, f32[2,288,896]{2,1,0:T(8,128)},...) custom-call(bf16[2,896,2304]{2,1,0:T(8,128)(2,1)} %wg.1, ...), custom_call_target="tpu_custom_call" | custom-call | tf_op jit(solution)/shard_map/train/pallas_call | solution.py:684
  337.7 25.9 %finish.1 = (bf16[2,896,2304]{2,1,0:T(8,128)(2,1)}, bf16[2,896,2304]{2,1,0:T(8,128)(2,1)}, bf16[2,8,288,896]{3,2,1,0:T(8,128)(2,1)}, f32[2,112,2304]{2,1,0:T(8,1...) custom-call(bf16[54,2,2,4,112,128]{5,4,3,2,1,0:T(8,128)(2,1)} %get-t, ...), custom_call_target="tpu_custom_call" | custom-call | tf_op jit(solution)/shard_map/finish/pallas_call | solution.py:807

commit v5 on v4

--- a/solution.py
+++ b/solution.py
@@ -20,12 +20,13 @@
 CHUNKS = 2 * PER_LAYER
 Q = 2 * CHUNKS
 LAG = 2
-HELD = 8
+HELD = 7
 RING = 2 * HELD
 SENDS = 4
+OUT = 3
 SPREAD = 4 + 6 * LAG
 LAST = Q + SPREAD + 3
-VMEM_LIMIT = 67043328
+VMEM_LIMIT = 48000000
 
 
 def nt(a, b):
@@ -46,10 +47,10 @@
 
 def train_kernel(
     wg, wu, wd, mg, mu, md, vg, vu, vd, x, dy,
-    wtmp, nmg, nmu, nmd, nvg, nvu, nvd, hid0_t, hid1_t, g0, u0, dg1, du1,
-    xv, dyv, av, at, gbuf, ubuf, dg, du, wgj, wuj, wdj, hid_b, hid_c,
-    grad, pin, rin, lin, rout, lout, news, gfin, mb, vb, wb, mbd, vbd, wbd,
-    load_sem, w_sem, gu_sem, keep_sem, hw_sem, hc_sem, d_sem, da_sem,
+    wtmp, nmg, nmu, nmd, nvg, nvu, nvd, hid0_t, hid1_t, dg1, du1,
+    xv, dyv, av, at, dg, du, wgj, wuj, wdj, hid_c,
+    grad, pin, sums_in, rout, lout, news, gfin, mb, vb, wb, mbd, vbd, wbd,
+    load_sem, w_sem, hw_sem, hc_sem, d_sem, da_sem,
     p_send, p_recv, r_send, r_recv, l_send, l_recv,
     or_send, or_recv, ol_send, ol_recv, ar_send, ar_recv, al_send, al_recv, ap_send, ap_recv, wo_sem, mo_sem, ad_sem,
 ):
@@ -82,12 +83,14 @@
         return remote(grad.at[e, 1 - c], pin.at[e], p_send.at[p % 2], p_recv.at[e], partner)
 
     def sum_right(q, frm):
-        part = pl.ds(frm + 1, 3 - frm)
-        return remote(rout.at[q % SENDS, part], rin.at[q % RING, part], r_send.at[q % SENDS], r_recv.at[q % RING], right)
+        part = pl.ds(frm, 3 - frm)
+        there = pl.ds(0, 3 - frm)
+        return remote(rout.at[q % OUT, part], sums_in.at[q % RING, there], r_send.at[q % OUT], r_recv.at[q % RING], right)
 
     def sum_left(q, frm):
         part = pl.ds(0, frm)
-        return remote(lout.at[q % SENDS, part], lin.at[q % RING, part], l_send.at[q % SENDS], l_recv.at[q % RING], left)
+        there = pl.ds(5 - frm, frm)
+        return remote(lout.at[q % OUT, part], sums_in.at[q % RING, there], l_send.at[q % OUT], l_recv.at[q % RING], left)
 
     def own_right(q, frm):
         here = news.at[q % RING, pl.ds(frm, 1)]
@@ -107,42 +110,47 @@
 
     def new_partner(q, core):
         return remote(
-            news.at[q % RING], wtmp.at[q // 2, core, q % 2], ap_send.at[q % SENDS], ap_recv.at[q % RING], partner
+            news.at[q % RING], wtmp.at[q // 2, core, q % 2], ap_send.at[q % 2], ap_recv.at[q % RING], partner
         )
 
     def keep_new(q):
-        return pltpu.make_async_copy(news.at[q % RING], wtmp.at[q // 2, c, q % 2], wo_sem.at[q % SENDS])
-
-    def moments(q, act, new=False):
-        p = q // 2
-        layer = jnp.where(p < PER_LAYER, 1, 0)
+        return pltpu.make_async_copy(news.at[q % RING], wtmp.at[q // 2, c, q % 2], wo_sem.at[q % 2])
+
+    def place(q):
+        p, s = q // 2, q % 2
         n = p % PER_LAYER
-        s = q % 2
         cols = pl.ds(pl.multiple_of((n // 2) * CF + s * LANES, LANES), LANES)
-        for which, (m, v, w, nm, nv) in enumerate(((mg, vg, wg, nmg, nvg), (mu, vu, wu, nmu, nvu))):
+        rows = pl.ds(pl.multiple_of(jnp.maximum(n - 18, 0) * OWN + s * HALF, HALF), HALF)
+        return jnp.where(p < PER_LAYER, 1, 0), n, s, cols, rows
+
+    def moments(q, act):
+        layer, n, s, cols, rows = place(q)
+        for which, (m, v, w) in enumerate(((mg, vg, wg), (mu, vu, wu))):
 
             @pl.when((n < 18) & (n % 2 == which))
             def _():
-                if new:
-                    act(pltpu.make_async_copy(mb.at[s], nm.at[layer, :, cols], mo_sem.at[s, 0]))
-                    act(pltpu.make_async_copy(vb.at[s], nv.at[layer, :, cols], mo_sem.at[s, 1]))
-                else:
-                    own = pl.ds(pl.multiple_of(me * ROWS, HALF), ROWS)
-                    act(pltpu.make_async_copy(m.at[layer, :, cols], mb.at[s], ad_sem.at[s, 0]))
-                    act(pltpu.make_async_copy(v.at[layer, :, cols], vb.at[s], ad_sem.at[s, 1]))
-                    act(pltpu.make_async_copy(w.at[layer, own, cols], wb.at[s], ad_sem.at[s, 2]))
+                own = pl.ds(pl.multiple_of(me * ROWS, HALF), ROWS)
+                act(pltpu.make_async_copy(m.at[layer, :, cols], mb.at[s], ad_sem.at[s, 0]))
+                act(pltpu.make_async_copy(v.at[layer, :, cols], vb.at[s], ad_sem.at[s, 1]))
+                act(pltpu.make_async_copy(w.at[layer, own, cols], wb.at[s], ad_sem.at[s, 2]))
 
         @pl.when(n >= 18)
         def _():
-            rows = pl.ds(pl.multiple_of((n - 18) * OWN + s * HALF, HALF), HALF)
-            if new:
-                act(pltpu.make_async_copy(mbd.at[s], nmd.at[layer, rows, :], mo_sem.at[s, 0]))
-                act(pltpu.make_async_copy(vbd.at[s], nvd.at[layer, rows, :], mo_sem.at[s, 1]))
-            else:
-                own = pl.ds(pl.multiple_of(me * 288 + (n - 18) * OWN + s * HALF, HALF), HALF)
-                act(pltpu.make_async_copy(md.at[layer, rows, :], mbd.at[s], ad_sem.at[s, 0]))
-                act(pltpu.make_async_copy(vd.at[layer, rows, :], vbd.at[s], ad_sem.at[s, 1]))
-                act(pltpu.make_async_copy(wd.at[layer, own, :], wbd.at[s], ad_sem.at[s, 2]))
+            own = pl.ds(pl.multiple_of(me * 288 + (n - 18) * OWN + s * HALF, HALF), HALF)
+            act(pltpu.make_async_copy(md.at[layer, rows, :], mbd.at[s], ad_sem.at[s, 0]))
+            act(pltpu.make_async_copy(vd.at[layer, rows, :], vbd.at[s], ad_sem.at[s, 1]))
+            act(pltpu.make_async_copy(wd.at[layer, own, :], wbd.at[s], ad_sem.at[s, 2]))
+
+    def keep_moments(q, act):
+        layer, n, s, cols, rows = place(q)
+
+        @pl.when((n < 18) & (n % 2 == 1))
+        def _():
+            act(pltpu.make_async_copy(vb.at[s], nvu.at[layer, :, cols], mo_sem.at[s]))
+
+        @pl.when(n >= 18)
+        def _():
+            act(pltpu.make_async_copy(vbd.at[s], nvd.at[layer, rows, :], mo_sem.at[s]))
 
     def adamw(w, m, v, g):
         m = 0.9 * m + 0.1 * g
@@ -155,33 +163,17 @@
         cols = pl.ds(pl.multiple_of((n % STEPS) * CF, CF), CF)
         layer = jnp.where((n >= STEPS) & (n < 2 * STEPS), 1, 0)
 
-        @pl.when(n < 2 * STEPS)
+        @pl.when(n < 3 * STEPS)
         def _():
             act(pltpu.make_async_copy(wg.at[layer, :, cols], wgj.at[s], w_sem.at[s, 0]))
             act(pltpu.make_async_copy(wu.at[layer, :, cols], wuj.at[s], w_sem.at[s, 1]))
-
-        @pl.when(n < 3 * STEPS)
-        def _():
             act(pltpu.make_async_copy(wd.at[layer, cols, :], wdj.at[s], w_sem.at[s, 2]))
-
-    def saved_of(j, act):
-        @pl.when(j < STEPS)
-        def _():
-            act(pltpu.make_async_copy(g0.at[j], gbuf, gu_sem.at[0]))
-            act(pltpu.make_async_copy(u0.at[j], ubuf, gu_sem.at[1]))
-
-    def keep_saved(j, r):
-        rows = pl.ds(pl.multiple_of(r * RB, RB), RB)
-        return (
-            pltpu.make_async_copy(gbuf.at[rows], g0.at[j, rows], keep_sem.at[r, 0]),
-            pltpu.make_async_copy(ubuf.at[rows], u0.at[j, rows], keep_sem.at[r, 1]),
-        )
 
     def keep_hidden0(j):
         return pltpu.make_async_copy(hid_c.at[j % 2], hid0_t.at[pl.ds(j * 8, 8)], hc_sem.at[j % 2])
 
     def keep_hidden(j):
-        return pltpu.make_async_copy(hid_b, hid1_t.at[pl.ds(j * 8, 8)], hw_sem)
+        return pltpu.make_async_copy(hid_c.at[1], hid1_t.at[pl.ds(j * 8, 8)], hw_sem)
 
     def keep_d(j):
         cols = pl.ds(pl.multiple_of(j * CF, CF), CF)
@@ -232,11 +224,44 @@
         for copy in halves:
             copy.start()
         load_dy.start()
+
         def normed_input(r):
+            halves[r].wait()
             wide = xv[rows_of(r), :].astype(F32)
             av[rows_of(r), :] = (wide * norm_scale(wide)).astype(BF16)
 
-        def output(r):
+        def step(j, first):
+            b = j % 2
+            weights_of(j + 1, start)
+            weights_of(j, wait)
+            if not first:
+
+                @pl.when(j > 1)
+                def _():
+                    keep_hidden0(j - 2).wait()
+
+            for r in range(NRB):
+                rows = rows_of(r)
+                a = av[rows, :]
+                g = nn(a, wgj[b])
+                u = nn(a, wuj[b])
+                hid = (g * sigmoid(g) * u).astype(BF16)
+                hid_c[b, :, :, rows] = hid.T.reshape(8, OWN, RB)
+                y = nn(hid, wdj[b])
+                acc[rows, :] = y if first else acc[rows, :] + y
+
+            keep_hidden0(j).start()
+
+        for r in range(NRB):
+            normed_input(r)
+        step(0, True)
+
+        @pl.loop(1, STEPS)
+        def _(j):
+            step(j, False)
+
+        @pl.loop(0, NRB)
+        def _(r):
             rows = rows_of(r)
             y = acc[rows, :].astype(BF16).astype(F32)
             h = (xv[rows, :].astype(F32) + y).astype(BF16)
@@ -244,55 +269,7 @@
             wide = h.astype(F32)
             av[rows, :] = (wide * norm_scale(wide)).astype(BF16)
 
-        def step(i, first, beside=None):
-            j, r = i // NRB, i % NRB
-            b = j % 2
-            rows = rows_of(r)
-
-            @pl.when(r == 0)
-            def _():
-                weights_of(j + 1, start)
-                weights_of(j, wait)
-
-                @pl.when(j > 1)
-                def _():
-                    keep_hidden0(j - 2).wait()
-
-            @pl.when(j > 0)
-            def _():
-                for copy in keep_saved(j - 1, r):
-                    copy.wait()
-
-            a = av[rows, :]
-            g = nn(a, wgj[b])
-            u = nn(a, wuj[b])
-            gbuf[rows, :] = g
-            ubuf[rows, :] = u
-            hid = (g * sigmoid(g) * u).astype(BF16)
-            hid_c[b, :, :, rows] = hid.T.reshape(8, OWN, RB)
-            y = nn(hid, wdj[b])
-            acc[rows, :] = y if first else acc[rows, :] + y
-            if beside:
-                beside()
-            for copy in keep_saved(j, r):
-                copy.start()
-
-            @pl.when(r == NRB - 1)
-            def _():
-                keep_hidden0(j).start()
-
-        halves[0].wait()
-        normed_input(0)
-        halves[1].wait()
-        step(0, True, lambda: normed_input(1))
-        step(1, True)
-
-        @pl.loop(NRB, NRB * STEPS - 1)
-        def _(i):
-            step(i, False)
-
-        step(NRB * STEPS - 1, False, lambda: output(0))
-        output(1)
+        keep_hidden0(STEPS - 2).wait()
         load_dy.wait()
 
     def first_layer(t):
@@ -319,7 +296,7 @@
             u = nn(a, wuj[b])
             dp = nt(dyv[rows, :], wdj[b]).astype(BF16).astype(F32)
             act, dgr, dur = hidden_back(g, u, dp)
-            hid_b[:, :, rows] = (act * u).astype(BF16).T.reshape(8, OWN, RB)
+            hid_c[1, :, :, rows] = (act * u).astype(BF16).T.reshape(8, OWN, RB)
             dg[rows, :] = dgr
             du[rows, :] = dur
 
@@ -339,20 +316,15 @@
                 keep_hidden(STEPS - 1).wait()
                 for copy in keep_d(STEPS - 1):
                     copy.wait()
-                for r in range(NRB):
-                    for copy in keep_saved(STEPS - 1, r):
-                        copy.wait()
-                for i in range(2):
-                    keep_hidden0(STEPS - 2 + i).wait()
+                keep_hidden0(STEPS - 1).wait()
                 hidden_of(hid1_t, 0, True)
-                saved_of(0, start)
-
-    def between(t, wgl, wul, dgb, dub, xb):
+
+    def between(t, wgl, wul, dgb, dub):
         k = (t - 36) // 2
         block = lambda i: (
             pltpu.make_async_copy(dg1.at[rows_of(i, CF)], dgb, da_sem.at[2]),
             pltpu.make_async_copy(du1.at[rows_of(i, CF)], dub, da_sem.at[3]),
-            pltpu.make_async_copy(x.at[rows_of(i, CF)], xb, da_sem.at[4]),
+            pltpu.make_async_copy(x.at[rows_of(i, CF)], av.at[rows_of(i, CF)], da_sem.at[4]),
         )
         weights = (
             pltpu.make_async_copy(wg.at[1], wgl, da_sem.at[0]),
@@ -383,8 +355,10 @@
             along = jnp.sum(da * wide, -1, keepdims=True) * (scale * scale * scale) * (-1.0 / D)
             back = (da * scale + wide * along).astype(BF16)
             xv[rows, :] = (dyv[rows, :].astype(F32) + back.astype(F32)).astype(BF16)
-            wide = xb[:].astype(F32)
-            at[:, rows] = (wide * norm_scale(wide)).astype(BF16).T
+            wide = av[rows, :].astype(F32)
+            a = (wide * norm_scale(wide)).astype(BF16)
+            av[rows, :] = a
+            at[:, rows] = a.T
 
             @pl.when(k < 8)
             def _():
@@ -410,19 +384,20 @@
         def _():
             weights_of(2 * STEPS + j + 1, start)
             weights_of(2 * STEPS + j, wait)
-            saved_of(j, wait)
 
         @pl.when((t < 90) & (turn < 2))
         def _():
             rows = rows_of(turn)
+            a = av[rows, :]
+            g = nn(a, wgj[b])
+            u = nn(a, wuj[b])
             dp = nt(xv[rows, :], wdj[b]).astype(BF16).astype(F32)
-            _, dgr, dur = hidden_back(gbuf[rows, :], ubuf[rows, :], dp)
+            _, dgr, dur = hidden_back(g, u, dp)
             dg[rows, :] = dgr
             du[rows, :] = dur
 
         @pl.when((t < 90) & (turn == 2))
         def _():
-            saved_of(j + 1, start)
             grad_columns(PER_LAYER + 2 * j, dg)
 
         @pl.when((t < 90) & (turn == 3))
@@ -475,15 +450,15 @@
                         sum_right(qr, zz - 1).wait_recv()
                     if zz < 3:
 
-                        @pl.when(qr >= SENDS)
+                        @pl.when(qr >= OUT)
                         def _():
-                            sum_right(qr - SENDS, zz).wait_send()
+                            sum_right(qr - OUT, zz).wait_send()
 
                         for to in range(zz + 1, 4):
                             total = own(qr, to)
                             if zz > 0:
-                                total = total + f32(rin[qr % RING, to])
-                            rout[qr % SENDS, to] = total.astype(BF16)
+                                total = total + f32(sums_in[qr % RING, to - zz])
+                            rout[qr % OUT, to - 1] = total.astype(BF16)
                         sum_right(qr, zz).start()
 
                 @pl.when(valid(ql))
@@ -492,15 +467,15 @@
                         sum_left(ql, zz + 1).wait_recv()
                     if zz > 0:
 
-                        @pl.when(ql >= SENDS)
+                        @pl.when(ql >= OUT)
                         def _():
-                            sum_left(ql - SENDS, zz).wait_send()
+                            sum_left(ql - OUT, zz).wait_send()
 
                         for to in range(zz):
                             total = own(ql, to)
                             if zz < 3:
-                                total = total + f32(lin[ql % RING, to])
-                            lout[ql % SENDS, to] = total.astype(BF16)
+                                total = total + f32(sums_in[ql % RING, 4 - zz + to])
+                            lout[ql % OUT, to] = total.astype(BF16)
                         sum_left(ql, zz).start()
 
     def optimizer(t):
@@ -508,7 +483,7 @@
 
         @pl.when((q >= 1) & (q <= Q))
         def _():
-            moments(q - 1, wait, new=True)
+            keep_moments(q - 1, wait)
 
         @pl.when(valid(q + 1))
         def _():
@@ -521,19 +496,24 @@
 
             @pl.when(z > 0)
             def _():
-                gfin[:] += f32(rin[q % RING, z])
+                gfin[:] += f32(sums_in[q % RING, 0])
 
             @pl.when(z < 3)
             def _():
-                gfin[:] += f32(lin[q % RING, z])
+                gfin[:] += f32(sums_in[q % RING, 4])
 
             moments(q, wait)
-            n = (q // 2) % PER_LAYER
-
-            @pl.when(n < 18)
+            layer, n, _, cols, rows = place(q)
+
+            @pl.when((n < 18) & (n % 2 == 0))
             def _():
                 g = f32(gfin[:].astype(BF16))
-                news[q % RING, z], mb[h], vb[h] = adamw(f32(wb[h]), mb[h], vb[h], g)
+                news[q % RING, z], nmg[layer, :, cols], nvg[layer, :, cols] = adamw(f32(wb[h]), mb[h], vb[h], g)
+
+            @pl.when((n < 18) & (n % 2 == 1))
+            def _():
+                g = f32(gfin[:].astype(BF16))
+                news[q % RING, z], nmu[layer, :, cols], vb[h] = adamw(f32(wb[h]), mb[h], vb[h], g)
 
             @pl.when(n >= 18)
             def _():
@@ -541,11 +521,11 @@
                     lanes = slice(i * LANES, (i + 1) * LANES)
                     part = slice(i * HALF, (i + 1) * HALF)
                     g = f32(gfin[part, :].astype(BF16))
-                    news[q % RING, z, part, :], mbd[h, :, lanes], vbd[h, :, lanes] = adamw(
+                    news[q % RING, z, part, :], nmd[layer, rows, lanes], vbd[h, :, lanes] = adamw(
                         f32(wbd[h, :, lanes]), mbd[h, :, lanes], vbd[h, :, lanes], g
                     )
 
-            moments(q, start, new=True)
+            keep_moments(q, start)
 
     def send(copy, q, frm):
         @pl.when(q >= SENDS)
@@ -601,10 +581,10 @@
 
         @pl.when(valid(q))
         def _():
-            @pl.when(q >= SENDS)
-            def _():
-                new_partner(q - SENDS, c).wait_send()
-                keep_new(q - SENDS).wait()
+            @pl.when(q >= 2)
+            def _():
+                new_partner(q - 2, c).wait_send()
+                keep_new(q - 2).wait()
 
             new_partner(q, c).start()
             keep_new(q).start()
@@ -616,19 +596,20 @@
     def last_waits():
         for i in range(2):
             to_partner(CHUNKS - 2 + i).wait_send()
-        for i in range(SENDS):
-            keep_new(Q - SENDS + i).wait()
-            new_partner(Q - SENDS + i, c).wait_send()
+            keep_new(Q - 2 + i).wait()
+            new_partner(Q - 2 + i, c).wait_send()
         for zz in range(4):
 
             @pl.when(z == zz)
             def _():
                 for q in range(Q - SENDS, Q):
                     if zz < 3:
-                        sum_right(q, zz).wait_send()
+                        if q >= Q - OUT:
+                            sum_right(q, zz).wait_send()
                         own_right(q, zz).wait_send()
                     if zz > 0:
-                        sum_left(q, zz).wait_send()
+                        if q >= Q - OUT:
+                            sum_left(q, zz).wait_send()
                         own_left(q, zz).wait_send()
                     if zz in (1, 2):
                         on_right(q, zz).wait_send()
@@ -653,6 +634,7 @@
             spread(t)
 
     pl.run_scoped(forward, pltpu.VMEM((T, D), F32))
+
     @pl.when((z == 0) | (z == 3))
     def _():
         pl.semaphore_wait(bar, 2)
@@ -664,8 +646,7 @@
     slots(0, 36, first_layer)
     pl.run_scoped(
         lambda *bufs: slots(36, 54, lambda t: between(t, *bufs)),
-        pltpu.VMEM((D, FF), BF16), pltpu.VMEM((D, FF), BF16),
-        pltpu.VMEM((CF, FF), BF16), pltpu.VMEM((CF, FF), BF16), pltpu.VMEM((CF, D), BF16),
+        pltpu.VMEM((D, FF), BF16), pltpu.VMEM((D, FF), BF16), pltpu.VMEM((CF, FF), BF16), pltpu.VMEM((CF, FF), BF16),
     )
     slots(54, LAST, last_layer)
     last_waits()
@@ -674,33 +655,33 @@
 def train(*operands):
     vm = pltpu.VMEM
     dma = pltpu.SemaphoreType.DMA
-    any_ = pl.BlockSpec(memory_space=pl.ANY)
+    any_, inside = pl.BlockSpec(memory_space=pl.ANY), pl.BlockSpec(memory_space=vm)
     shape = jax.ShapeDtypeStruct
     out_shape = [
         shape((CHUNKS, 2, 2, 4, ROWS, LANES), BF16), *[shape(t.shape, F32) for t in operands[3:9]],
         shape((72, OWN, T), BF16), shape((72, OWN, T), BF16),
-        shape((STEPS, T, CF), F32), shape((STEPS, T, CF), F32), shape((T, FF), BF16), shape((T, FF), BF16),
+        shape((T, FF), BF16), shape((T, FF), BF16),
     ]
     return pl.pallas_call(
         train_kernel,
         in_specs=[any_] * len(operands),
-        out_specs=[any_] * len(out_shape),
+        out_specs=[any_, *[inside] * 4, *[any_] * (len(out_shape) - 5)],
         out_shape=out_shape,
         scratch_shapes=[
             vm((T, D), BF16), vm((T, D), BF16), vm((T, D), BF16), vm((D, T), BF16),
-            vm((T, CF), F32), vm((T, CF), F32), vm((T, CF), BF16), vm((T, CF), BF16),
+            vm((T, CF), BF16), vm((T, CF), BF16),
             vm((2, D, CF), BF16), vm((2, D, CF), BF16), vm((2, CF, D), BF16),
-            vm((8, OWN, T), BF16), vm((2, 8, OWN, T), BF16),
+            vm((2, 8, OWN, T), BF16),
             vm((HELD, 2, 2, 4, ROWS, LANES), BF16), vm((HELD, 2, 4, ROWS, LANES), BF16),
-            vm((RING, 4, ROWS, LANES), BF16), vm((RING, 4, ROWS, LANES), BF16),
-            vm((SENDS, 4, ROWS, LANES), BF16), vm((SENDS, 4, ROWS, LANES), BF16),
+            vm((RING, 5, ROWS, LANES), BF16),
+            vm((OUT, 3, ROWS, LANES), BF16), vm((OUT, 3, ROWS, LANES), BF16),
             vm((RING, 4, ROWS, LANES), BF16), vm((ROWS, LANES), F32),
             vm((2, ROWS, LANES), F32), vm((2, ROWS, LANES), F32), vm((2, ROWS, LANES), BF16),
             vm((2, HALF, D), F32), vm((2, HALF, D), F32), vm((2, HALF, D), BF16),
-            dma((3,)), dma((2, 3)), dma((2,)), dma((NRB, 2)), dma, dma((2,)), dma((2,)), dma((5,)),
+            dma((3,)), dma((2, 3)), dma, dma((2,)), dma((2,)), dma((5,)),
             dma((2,)), dma((HELD,)), dma((SENDS,)), dma((RING,)), dma((SENDS,)), dma((RING,)),
             dma((SENDS,)), dma((RING,)), dma((SENDS,)), dma((RING,)), dma((SENDS,)), dma((RING,)),
-            dma((SENDS,)), dma((RING,)), dma((SENDS,)), dma((RING,)), dma((SENDS,)), dma((2, 2)), dma((2, 3)),
+            dma((SENDS,)), dma((RING,)), dma((SENDS,)), dma((RING,)), dma((SENDS,)), dma((2,)), dma((2, 3)),
         ],
         compiler_params=pltpu.CompilerParams(
             collective_id=0, has_side_effects=True, vmem_limit_bytes=VMEM_LIMIT
@@ -714,19 +695,19 @@
 
 def finish_kernel(
     wt, mg, mu, md, vg, vu, vd, owg, owu, owd, omg, omu, omd, ovg, ovu, ovd,
-    wv, mgv, muv, mdv, vgv, vuv, vdv, columns, rows, w_sem, in_sem, out_sem, col_sem, row_sem,
+    wv, vuv, vdv, columns, rows, w_sem, in_sem, out_sem, col_sem, row_sem,
 ):
-    moments = ((mg, mgv, omg), (mu, muv, omu), (md, mdv, omd), (vg, vgv, ovg), (vu, vuv, ovu), (vd, vdv, ovd))
+    moments = ((mg, omg), (mu, omu), (md, omd), (vg, ovg), (vuv, ovu), (vdv, ovd))
     pieces = [(i, layer) for layer in (1, 0) for i in range(6)]
 
-    def take(i, layer):
-        return pltpu.make_async_copy(moments[i][0].at[layer], moments[i][1].at[layer], in_sem.at[i, layer])
+    def take(layer):
+        return [pltpu.make_async_copy(a.at[layer], b.at[layer], in_sem.at[i, layer]) for i, (a, b) in enumerate(((vu, vuv), (vd, vdv)))]
 
     def give(i, layer):
-        return pltpu.make_async_copy(moments[i][1].at[layer], moments[i][2].at[layer], out_sem.at[i, layer])
+        return pltpu.make_async_copy(moments[i][0].at[layer], moments[i][1].at[layer], out_sem.at[i, layer])
 
     def chunk(p):
-        return pltpu.make_async_copy(wt.at[p], wv.at[p], w_sem.at[p])
+        return pltpu.make_async_copy(wt.at[p], wv.at[p % (AHEAD + 1)], w_sem.at[p % (AHEAD + 1)])
 
     def columns_out(out, layer, j, b):
         return pltpu.make_async_copy(columns.at[b], out.at[layer, :, pl.ds(pl.multiple_of(j * CF, CF), CF)], col_sem.at[b])
@@ -736,8 +717,6 @@
 
     for p in range(AHEAD):
         chunk(p).start()
-    for i in range(2):
-        take(*pieces[i]).start()
 
     def chunk_in(p):
         @pl.when(p + AHEAD < CHUNKS)
@@ -754,6 +733,7 @@
             n = n0 + i
             p = base + n
             chunk_in(p)
+            e = p % (AHEAD + 1)
             if n0 < 18:
                 b = n % 4
 
@@ -763,7 +743,7 @@
 
                 for o in range(8):
                     for h in range(2):
-                        columns[b, o * ROWS : (o + 1) * ROWS, h * LANES : (h + 1) * LANES] = wv[p, o % 2, h, o // 2]
+                        columns[b, o * ROWS : (o + 1) * ROWS, h * LANES : (h + 1) * LANES] = wv[e, o % 2, h, o // 2]
 
                 @pl.when(n % 2 == 0)
                 def _():
@@ -784,15 +764,19 @@
                     for h in range(2):
                         for c in range(7):
                             rows[b, o, h * HALF : (h + 1) * HALF, c * LANES : (c + 1) * LANES] = wv[
-                                p, o % 2, h, o // 2, c * HALF : (c + 1) * HALF, :
+                                e, o % 2, h, o // 2, c * HALF : (c + 1) * HALF, :
                             ]
                 rows_out(layer, k, b).start()
 
         if part < 12:
-            take(*pieces[part]).wait()
-            give(*pieces[part]).start()
-            if part + 2 < 12:
-                take(*pieces[part + 2]).start()
+            piece, side = pieces[part], part % 6
+            if side == 0:
+                for copy in take(piece[1]):
+                    copy.start()
+            if side == 4:
+                for copy in take(piece[1]):
+                    copy.wait()
+            give(*piece).start()
 
     for b in range(4):
         columns_out(owg, 0, 0, b).wait()
@@ -803,10 +787,10 @@
 
 def finish(wtmp, *moments):
     vm, dma = pltpu.VMEM, pltpu.SemaphoreType.DMA
-    any_ = pl.BlockSpec(memory_space=pl.ANY)
+    any_, inside = pl.BlockSpec(memory_space=pl.ANY), pl.BlockSpec(memory_space=vm)
     out = pl.pallas_call(
         finish_kernel,
-        in_specs=[any_] * 7,
+        in_specs=[any_, *[inside] * 4, any_, any_],
         out_specs=[any_] * 9,
         out_shape=[
             jax.ShapeDtypeStruct((2, D, FF), BF16), jax.ShapeDtypeStruct((2, D, FF), BF16),
@@ -814,10 +798,11 @@
             *[jax.ShapeDtypeStruct(t.shape, F32) for t in moments],
         ],
         scratch_shapes=[
-            vm(wtmp.shape, BF16), *[vm(t.shape, F32) for t in moments], vm((4, D, CF), BF16), vm((4, 8, OWN, D), BF16),
-            dma((CHUNKS,)), dma((6, 2)), dma((6, 2)), dma((4,)), dma((4,)),
+            vm((AHEAD + 1, *wtmp.shape[1:]), BF16), vm(moments[4].shape, F32), vm(moments[5].shape, F32),
+            vm((4, D, CF), BF16), vm((4, 8, OWN, D), BF16),
+            dma((AHEAD + 1,)), dma((2, 2)), dma((6, 2)), dma((4,)), dma((4,)),
         ],
-        compiler_params=pltpu.CompilerParams(vmem_limit_bytes=VMEM_LIMIT),
+        compiler_params=pltpu.CompilerParams(vmem_limit_bytes=48000000),
         name="finish",
     )(wtmp, *moments)
     return (out[0], out[1], out[2].reshape(2, FF, D), *out[3:])

time: 364 us -> 360 us (0.989)
  Pallas kernels: 363 us -> 359 us
where the time goes in v5:
time: 360 us
  Pallas kernels  359 us (100%)
    pallas_call x1, Pallas kernels, train(): pl.pallas_call(train_kernel, in_specs=[any_] * len(operands), out_specs=[...  337 us
    pallas_call x1, Pallas kernels, finish(): pl.pallas_call(finish_kernel, in_specs=[any_, *[inside] * 4, any_, any_],...  22.3 us

profile of v5, /device:TPU:0, one launch (start us, length us, event | category | flops | bytes accessed | tf_op | source)
XLA Modules:
  0.0 359.7 jit_solution(16107096170824697798)
XLA Ops:
  0.6 336.5 %train.1 = (bf16[54,2,2,4,112,128]{5,4,3,2,1,0:T(8,128)(2,1)}, f32[2,112,2304]{2,1,0:T(8,128)S(1)}, f32[2,112,2304]{2,1,0:T(8,128)S(1)}, f32[2,288,896]{2,1,0:T(...) custom-call(bf16[2,896,2304]{2,1,0:T(8,128)(2,1)} %wg.1, ...), custom_call_target="tpu_custom_call" | custom-call | tf_op jit(solution)/shard_map/train/pallas_call | solution.py:665
  337.2 22.3 %finish.1 = (bf16[2,896,2304]{2,1,0:T(8,128)(2,1)}, bf16[2,896,2304]{2,1,0:T(8,128)(2,1)}, bf16[2,8,288,896]{3,2,1,0:T(8,128)(2,1)}, f32[2,112,2304]{2,1,0:T(8,1...) custom-call(bf16[54,2,2,4,112,128]{5,4,3,2,1,0:T(8,128)(2,1)} %get-t, ...), custom_call_target="tpu_custom_call" | custom-call | tf_op jit(solution)/shard_map/finish/pallas_call | solution.py:791

commit v6 on v5

--- a/solution.py
+++ b/solution.py
@@ -20,7 +20,7 @@
 CHUNKS = 2 * PER_LAYER
 Q = 2 * CHUNKS
 LAG = 2
-HELD = 7
+HELD = 8
 RING = 2 * HELD
 SENDS = 4
 OUT = 3
@@ -110,11 +110,11 @@
 
     def new_partner(q, core):
         return remote(
-            news.at[q % RING], wtmp.at[q // 2, core, q % 2], ap_send.at[q % 2], ap_recv.at[q % RING], partner
+            news.at[q % RING], wtmp.at[q // 2, core, q % 2], ap_send.at[q % SENDS], ap_recv.at[q % RING], partner
         )
 
     def keep_new(q):
-        return pltpu.make_async_copy(news.at[q % RING], wtmp.at[q // 2, c, q % 2], wo_sem.at[q % 2])
+        return pltpu.make_async_copy(news.at[q % RING], wtmp.at[q // 2, c, q % 2], wo_sem.at[q % SENDS])
 
     def place(q):
         p, s = q // 2, q % 2
@@ -581,10 +581,10 @@
 
         @pl.when(valid(q))
         def _():
-            @pl.when(q >= 2)
-            def _():
-                new_partner(q - 2, c).wait_send()
-                keep_new(q - 2).wait()
+            @pl.when(q >= SENDS)
+            def _():
+                new_partner(q - SENDS, c).wait_send()
+                keep_new(q - SENDS).wait()
 
             new_partner(q, c).start()
             keep_new(q).start()
@@ -596,8 +596,9 @@
     def last_waits():
         for i in range(2):
             to_partner(CHUNKS - 2 + i).wait_send()
-            keep_new(Q - 2 + i).wait()
-            new_partner(Q - 2 + i, c).wait_send()
+        for i in range(SENDS):
+            keep_new(Q - SENDS + i).wait()
+            new_partner(Q - SENDS + i, c).wait_send()
         for zz in range(4):
 
             @pl.when(z == zz)

time: 360 us -> 359 us (level)
  no operation moved by 1% of the time
where the time goes in v6:
time: 359 us
  Pallas kernels  358 us (100%)
    pallas_call x1, Pallas kernels, train(): pl.pallas_call(train_kernel, in_specs=[any_] * len(operands), out_specs=[...  336 us
    pallas_call x1, Pallas kernels, finish(): pl.pallas_call(finish_kernel, in_specs=[any_, *[inside] * 4, any_, any_],...  22.3 us

profile of v6, /device:TPU:0, one launch (start us, length us, event | category | flops | bytes accessed | tf_op | source)
XLA Modules:
  0.0 358.8 jit_solution(6059433768771704770)
XLA Ops:
  0.6 335.7 %train.1 = (bf16[54,2,2,4,112,128]{5,4,3,2,1,0:T(8,128)(2,1)}, f32[2,112,2304]{2,1,0:T(8,128)S(1)}, f32[2,112,2304]{2,1,0:T(8,128)S(1)}, f32[2,288,896]{2,1,0:T(...) custom-call(bf16[2,896,2304]{2,1,0:T(8,128)(2,1)} %wg.1, ...), custom_call_target="tpu_custom_call" | custom-call | tf_op jit(solution)/shard_map/train/pallas_call | solution.py:666
  336.3 22.3 %finish.1 = (bf16[2,896,2304]{2,1,0:T(8,128)(2,1)}, bf16[2,896,2304]{2,1,0:T(8,128)(2,1)}, bf16[2,8,288,896]{3,2,1,0:T(8,128)(2,1)}, f32[2,112,2304]{2,1,0:T(8,1...) custom-call(bf16[54,2,2,4,112,128]{5,4,3,2,1,0:T(8,128)(2,1)} %get-t, ...), custom_call_target="tpu_custom_call" | custom-call | tf_op jit(solution)/shard_map/finish/pallas_call | solution.py:792
